TPU v7x, 16 devices: a whole 2x2x2 slice. The times are simulated.
16 devices in a mesh: replica: 2 (over z), model: 8 (over y, x, core).
Axes of the slice: x: 2, y: 2, z: 2, core: 2. Of those that a mesh axis runs over, the one named last changes fastest.
Arguments:
- prompt: bfloat16 [16, 1536, 2048], P('replica', 'model'), parts along dimension 0
- lengths: int32 [16], P('replica'), parts along dimension 0
- new_tok: bfloat16 [16, 2048], P('replica'), parts along dimension 0
- norm_attn: bfloat16 [1, 2048], replicated
- w_q: bfloat16 [1, 2048, 2048], P(None, None, 'model')
- w_k: bfloat16 [1, 2048, 2048], P(None, None, 'model')
- w_v: bfloat16 [1, 2048, 2048], P(None, None, 'model')
- w_o: bfloat16 [1, 2048, 2048], P(None, 'model')
- norm_mlp: bfloat16 [1, 2048], replicated
- w_gate: bfloat16 [1, 2048, 8192], P(None, None, 'model')
- w_up: bfloat16 [1, 2048, 8192], P(None, None, 'model')
- w_down: bfloat16 [1, 8192, 2048], P(None, 'model')
Outputs:
- output 1: bfloat16 [16, 2048], P('replica'), parts along dimension 0
- output 2: bfloat16 [16, 2048], P('replica'), parts along dimension 0
- output 3: bfloat16 [1, 16, 1537, 16, 128], P(None, 'replica', None, 'model'), parts along dimension 1
- output 4: bfloat16 [1, 16, 1537, 16, 128], P(None, 'replica', None, 'model'), parts along dimension 1
There are 2 independent parts. A program takes and returns all parts, laid end to end along the dimension named above; an argument that names none is the same for every part.
All inputs are finite; a program needn't handle non-finite values.
Results may differ from a plain program's by a relative error of at most 0.0109076.
Values are sent between devices in bfloat16 or wider.
A program may use at most 1 GiB of HBM per device.

v0:
```python
import jax
import jax.numpy as jnp
from jax import lax
from jax.sharding import PartitionSpec as P

HEAD_DIM = 128
NEG_BIG = -1e30


def rms_norm(hidden, gain_vec):
    hid_f32 = hidden.astype(jnp.float32)
    inv_rms = lax.rsqrt(jnp.mean(hid_f32 * hid_f32, axis=-1, keepdims=True) + 1e-5)
    return (hid_f32 * inv_rms * gain_vec.astype(jnp.float32)).astype(jnp.bfloat16)


def rotary(heads_f32, positions):
    half_dim = HEAD_DIM // 2
    inv_freq = 10000.0 ** (-2.0 * jnp.arange(half_dim, dtype=jnp.float32) / HEAD_DIM)
    angles = positions.astype(jnp.float32)[..., None] * inv_freq
    cos_tab = jnp.cos(angles)[..., None, :]
    sin_tab = jnp.sin(angles)[..., None, :]
    lo_half = heads_f32[..., :half_dim]
    hi_half = heads_f32[..., half_dim:]
    return jnp.concatenate([lo_half * cos_tab - hi_half * sin_tab, hi_half * cos_tab + lo_half * sin_tab], axis=-1)


def block_attention(q_block, key_blocks, val_blocks, lengths, q_start, n_used):
    n_batch, blk_len, n_heads, _ = q_block.shape
    kv_heads = key_blocks.shape[3]
    n_group = n_heads // kv_heads
    q_grouped = q_block.reshape(n_batch, blk_len, kv_heads, n_group, HEAD_DIM)
    q_pos = q_start + jnp.arange(blk_len)
    score_scale = HEAD_DIM ** -0.5

    def step_fn(blk_idx, loop_state):
        run_max, run_sum, run_acc = loop_state
        key_blk = lax.dynamic_index_in_dim(key_blocks, blk_idx, axis=0, keepdims=False)
        val_blk = lax.dynamic_index_in_dim(val_blocks, blk_idx, axis=0, keepdims=False)
        k_pos = blk_idx * blk_len + jnp.arange(blk_len)
        scores = jnp.einsum('bqhgd,bkhd->bqhgk', q_grouped, key_blk, preferred_element_type=jnp.float32) * score_scale
        visible = (k_pos[None, None, :] <= q_pos[None, :, None]) & (k_pos[None, None, :] < lengths[:, None, None])
        scores = jnp.where(visible[:, :, None, None, :], scores, NEG_BIG)
        new_max = jnp.maximum(run_max, jnp.max(scores, axis=-1))
        rescale = jnp.exp(run_max - new_max)
        attn_prob = jnp.exp(scores - new_max[..., None])
        run_sum = run_sum * rescale + jnp.sum(attn_prob, axis=-1)
        run_acc = run_acc * rescale[..., None] + jnp.einsum('bqhgk,bkhd->bqhgd', attn_prob.astype(jnp.bfloat16), val_blk, preferred_element_type=jnp.float32)
        return new_max, run_sum, run_acc

    stat_shape = (n_batch, blk_len, kv_heads, n_group)
    init_state = (jnp.full(stat_shape, NEG_BIG, jnp.float32), jnp.zeros(stat_shape, jnp.float32), jnp.zeros(stat_shape + (HEAD_DIM,), jnp.float32))
    run_max, run_sum, run_acc = lax.fori_loop(0, n_used, step_fn, init_state)
    return (run_acc / run_sum[..., None]).reshape(n_batch, blk_len, n_heads * HEAD_DIM).astype(jnp.bfloat16)


def decode_attention(q_new, key_cache, val_cache, lengths):
    n_batch, n_heads, _ = q_new.shape
    kv_heads = key_cache.shape[2]
    cache_len = key_cache.shape[1]
    q_grouped = q_new.reshape(n_batch, kv_heads, n_heads // kv_heads, HEAD_DIM)
    scores = jnp.einsum('bhgd,bkhd->bhgk', q_grouped, key_cache, preferred_element_type=jnp.float32) * (HEAD_DIM ** -0.5)
    cache_pos = jnp.arange(cache_len)
    visible = (cache_pos[None, :] < lengths[:, None]) | (cache_pos[None, :] == cache_len - 1)
    scores = jnp.where(visible[:, None, None, :], scores, NEG_BIG)
    attn_prob = jax.nn.softmax(scores, axis=-1)
    out_f32 = jnp.einsum('bhgk,bkhd->bhgd', attn_prob.astype(jnp.bfloat16), val_cache, preferred_element_type=jnp.float32)
    return out_f32.reshape(n_batch, n_heads * HEAD_DIM).astype(jnp.bfloat16)


def decode_layer(dec_hidden, key_mine, val_mine, lengths, gain_attn, wq_loc, wk_loc, wv_loc, wo_loc, gain_mlp, wg_loc, wu_loc, wd_loc):
    n_batch = dec_hidden.shape[0]
    heads_loc = wq_loc.shape[1] // HEAD_DIM
    kv_loc = wk_loc.shape[1] // HEAD_DIM
    tok_norm = rms_norm(dec_hidden, gain_attn)
    q_new = rotary(jnp.dot(tok_norm, wq_loc, preferred_element_type=jnp.float32).reshape(n_batch, heads_loc, HEAD_DIM), lengths).astype(jnp.bfloat16)
    k_new = rotary(jnp.dot(tok_norm, wk_loc, preferred_element_type=jnp.float32).reshape(n_batch, kv_loc, HEAD_DIM), lengths).astype(jnp.bfloat16)
    v_new = jnp.dot(tok_norm, wv_loc, preferred_element_type=jnp.float32).astype(jnp.bfloat16).reshape(n_batch, kv_loc, HEAD_DIM)
    key_cache = jnp.concatenate([key_mine, k_new[:, None]], axis=1)
    val_cache = jnp.concatenate([val_mine, v_new[:, None]], axis=1)
    tok_attn = decode_attention(q_new, key_cache, val_cache, lengths)
    attn_part = jnp.dot(tok_attn, wo_loc, preferred_element_type=jnp.float32)
    dec_hidden = (dec_hidden.astype(jnp.float32) + lax.psum(attn_part, 'model')).astype(jnp.bfloat16)
    tok_norm = rms_norm(dec_hidden, gain_mlp)
    tok_mid = (jax.nn.silu(jnp.dot(tok_norm, wg_loc, preferred_element_type=jnp.float32)) * jnp.dot(tok_norm, wu_loc, preferred_element_type=jnp.float32)).astype(jnp.bfloat16)
    mlp_part = jnp.dot(tok_mid, wd_loc, preferred_element_type=jnp.float32)
    dec_hidden = (dec_hidden.astype(jnp.float32) + lax.psum(mlp_part, 'model')).astype(jnp.bfloat16)
    return dec_hidden, key_cache, val_cache


def solution(mesh):
    n_dev = mesh.shape['model']
    seq_spec = P('replica', 'model', None)
    col_spec = P(None, None, 'model')
    row_spec = P(None, 'model', None)
    gain_spec = P(None, None)
    tok_spec = P('replica', None)
    cache_spec = P(None, 'replica', None, 'model', None)
    in_specs = (seq_spec, P('replica'), tok_spec, gain_spec, col_spec, col_spec, col_spec, row_spec, gain_spec, col_spec, col_spec, row_spec)
    out_specs = (tok_spec, tok_spec, cache_spec, cache_spec)

    def per_device(prompt, lengths, new_tok, norm_attn, w_q, w_k, w_v, w_o, norm_mlp, w_gate, w_up, w_down):
        my_idx = lax.axis_index('model')
        n_batch, seq_loc, d_model = prompt.shape
        n_tok = n_batch * seq_loc
        kv_loc = w_k.shape[2] // HEAD_DIM
        n_heads = (w_q.shape[2] // HEAD_DIM) * n_dev
        kv_heads = kv_loc * n_dev
        seq_len = seq_loc * n_dev
        seq_pos = my_idx * seq_loc + jnp.arange(seq_loc)
        hidden = prompt
        dec_hidden = new_tok
        key_layers = []
        val_layers = []
        for layer_idx in range(w_q.shape[0]):
            wq_full = lax.all_gather(w_q[layer_idx], 'model', axis=1, tiled=True)
            wk_full = lax.all_gather(w_k[layer_idx], 'model', axis=1, tiled=True)
            wv_full = lax.all_gather(w_v[layer_idx], 'model', axis=1, tiled=True)
            wo_full = lax.all_gather(w_o[layer_idx], 'model', axis=0, tiled=True)
            wg_full = lax.all_gather(w_gate[layer_idx], 'model', axis=1, tiled=True)
            wu_full = lax.all_gather(w_up[layer_idx], 'model', axis=1, tiled=True)
            wd_full = lax.all_gather(w_down[layer_idx], 'model', axis=0, tiled=True)
            normed = rms_norm(hidden, norm_attn[layer_idx]).reshape(n_tok, d_model)
            q_rot = rotary(jnp.dot(normed, wq_full, preferred_element_type=jnp.float32).reshape(n_batch, seq_loc, n_heads, HEAD_DIM), seq_pos).astype(jnp.bfloat16)
            k_rot = rotary(jnp.dot(normed, wk_full, preferred_element_type=jnp.float32).reshape(n_batch, seq_loc, kv_heads, HEAD_DIM), seq_pos).astype(jnp.bfloat16)
            v_proj = jnp.dot(normed, wv_full, preferred_element_type=jnp.float32).astype(jnp.bfloat16).reshape(n_batch, seq_loc, kv_heads, HEAD_DIM)
            key_blocks = lax.all_gather(k_rot, 'model', axis=0)
            val_blocks = lax.all_gather(v_proj, 'model', axis=0)
            attn_out = block_attention(q_rot, key_blocks, val_blocks, lengths, my_idx * seq_loc, my_idx + 1).reshape(n_tok, n_heads * HEAD_DIM)
            hidden = (hidden.astype(jnp.float32) + jnp.dot(attn_out, wo_full, preferred_element_type=jnp.float32).reshape(n_batch, seq_loc, d_model)).astype(jnp.bfloat16)
            normed = rms_norm(hidden, norm_mlp[layer_idx]).reshape(n_tok, d_model)
            mlp_mid = (jax.nn.silu(jnp.dot(normed, wg_full, preferred_element_type=jnp.float32)) * jnp.dot(normed, wu_full, preferred_element_type=jnp.float32)).astype(jnp.bfloat16)
            hidden = (hidden.astype(jnp.float32) + jnp.dot(mlp_mid, wd_full, preferred_element_type=jnp.float32).reshape(n_batch, seq_loc, d_model)).astype(jnp.bfloat16)
            key_mine = jnp.moveaxis(lax.dynamic_slice_in_dim(key_blocks, my_idx * kv_loc, kv_loc, axis=3), 0, 1).reshape(n_batch, seq_len, kv_loc, HEAD_DIM)
            val_mine = jnp.moveaxis(lax.dynamic_slice_in_dim(val_blocks, my_idx * kv_loc, kv_loc, axis=3), 0, 1).reshape(n_batch, seq_len, kv_loc, HEAD_DIM)
            dec_hidden, key_cache, val_cache = decode_layer(dec_hidden, key_mine, val_mine, lengths, norm_attn[layer_idx], w_q[layer_idx], w_k[layer_idx], w_v[layer_idx], w_o[layer_idx], norm_mlp[layer_idx], w_gate[layer_idx], w_up[layer_idx], w_down[layer_idx])
            key_layers.append(key_cache)
            val_layers.append(val_cache)
        last_sel = (seq_pos[None, :] == (lengths - 1)[:, None]).astype(jnp.bfloat16)
        last_part = jnp.einsum('bs,bsd->bd', last_sel, hidden, preferred_element_type=jnp.float32)
        last_hidden = lax.psum(last_part, 'model').astype(jnp.bfloat16)
        return dec_hidden, last_hidden, jnp.stack(key_layers), jnp.stack(val_layers)

    return jax.shard_map(per_device, mesh=mesh, in_specs=in_specs, out_specs=out_specs, check_vma=False)
```

profile of v0, /device:TPU:0, one launch (start us, length us, event | category | flops | bytes accessed | tf_op | source)
XLA Modules:
  0.0 1558.6 jit_solution(13656497704972601655)
XLA Ops:
  18.8 45.7 %all-gather.23.cloned.1.call-done = bf16[1,2048,2048]{2,1,0:T(8,128)(2,1)} async-done(((bf16[1,2048,256]{2,1,0:T(8,128)(2,1)}), bf16[1,2048,2048]{2,1,0:T(8,128)(2,1)}) %all-gather.23.cloned.1.call-update) | async-done | bytes 8388624 | tf_op jit(solution)/shard_map/all_gather | solution.py:117
  64.4 17.4 %fusion.65 = bf16[192,8,16,128]{3,1,2,0:T(8,128)(2,1)S(1)} fusion(bf16[1536,2048]{1,0:T(8,128)(2,1)} %bitcast.242, bf16[1,2048,2048]{2,1,0:T(8,128)(2,1)} %all-gather.23.cloned.1.call-done), kind=kOutput, calls=%fused_computation.85 | convolution fusion | flops 12888047616 | bytes 20971520 | tf_op jit(solution)/shard_map/dot_general | solution.py:125
  87.8 30.2 %all-gather.25.cloned.1.call-done = bf16[1,2048,2048]{2,1,0:T(8,128)(2,1)} async-done(((bf16[1,2048,256]{2,1,0:T(8,128)(2,1)}), bf16[1,2048,2048]{2,1,0:T(8,128)(2,1)}) %all-gather.25.cloned.1.call-update) | async-done | bytes 8388624 | tf_op jit(solution)/shard_map/all_gather | solution.py:115
  118.1 12.3 copy.74
  130.4 41.3 %all-gather.21.cloned.1.call-done = bf16[1,2048,2048]{2,1,0:T(8,128)(2,1)} async-done(((bf16[1,2048,256]{2,1,0:T(8,128)(2,1)}), bf16[1,2048,2048]{2,1,0:T(8,128)(2,1)}) %all-gather.21.cloned.1.call-update) | async-done | bytes 8388624 | tf_op jit(solution)/shard_map/all_gather | solution.py:116
  171.7 12.5 copy.67
  184.2 19.6 %fusion.49 = f32[8,192,16,128]{3,1,2,0:T(8,128)} fusion(bf16[16,128,2048,1]{2,1,0,3:T(8,128)(2,1)} %bitcast.239, bf16[8,192,2048]{2,1,0:T(8,128)(2,1)} %fusion.30), kind=kOutput, calls=%fused_computation.71 | convolution fusion | flops 12884901888 | bytes 27262976 | tf_op jit(solution)/shard_map/dot_general | solution.py:123
  203.8 15.6 fusion.51
  219.4 27.8 %fusion.45 = (bf16[8,192,16,1,64]{4,1,2,0,3:T(8,128)(2,1)}, bf16[8,192,16,1,64]{4,1,2,0,3:T(8,128)(2,1)}, bf16[1,8,192,16,64]{4,2,3,1,0:T(8,128)(2,1)}, bf16[1,8,192,16,64]{4,2,3,1,0:T(8,128)(2,1)}) fusion(f32[8,192,16,128]{3,1,2,0:T(8,128)} %fusion.49, f32[192,64]{1,0:T(8,128)S(1)} %get-tuple-element.173, f32[192,64]{1,0:T(8,128)S(1)} %get-tuple-element.172, ...), kind=kLoop, calls=%fused_computation.66 | loop fusion | flops 25165824 | bytes 37847040 | tf_op jit(solution)/shard_map/concatenate | solution.py:24
  272.7 9.7 pad_maximum_fusion.3
  282.4 120.1 %all-gather.19.cloned.1.call-done = bf16[8,8,192,16,128]{4,3,2,1,0:T(8,128)(2,1)} async-done(((bf16[1,8,192,16,128]{4,3,2,1,0:T(8,128)(2,1)}), bf16[8,8,192,16,128]{4,3,2,1,0:T(8,128)(2,1)}) %all-gather.19.cloned.1.call-update) | async-done | bytes 50331664 | tf_op jit(solution)/shard_map/all_gather | solution.py:127
  402.5 230.2 %all-gather.17.cloned.1.call-done = bf16[8,8,192,16,128]{4,3,2,1,0:T(8,128)(2,1)} async-done(((bf16[1,8,192,16,128]{4,3,2,1,0:T(8,128)(2,1)}), bf16[8,8,192,16,128]{4,3,2,1,0:T(8,128)(2,1)}) %all-gather.17.cloned.1.call-update) | async-done | bytes 50331664 | tf_op jit(solution)/shard_map/all_gather | solution.py:126
  632.7 27.5 %constant_dynamic-slice_fusion.2 = (bf16[8,8,192,2,128]{4,3,2,1,0:T(2,128)(2,1)}, bf16[8,8,192,2,128]{4,3,2,1,0:T(2,128)(2,1)}) fusion(bf16[8,8,192,16,128]{4,3,2,1,0:T(8,128)(2,1)} %all-gather.19.cloned.1.call-done, s32[]{:T(128)S(6)} %select_n.18, bf16[8,8,192,16,128]{4,3,2,1,0:T(8,128)(2,1)} %all-gather.17.cloned.1.call-done), kind=kLoop, calls=%fused_computation.155 | loop fusion | bytes 25165828 | tf_op jit(solution)/shard_map/dynamic_slice | solution.py:134
  660.1 7.2 copy.93
  677.8 61.9 %while.15 = (s32[]{:T(128)}, f32[8,192,16,1]{1,2,0,3:T(8,128)S(1)}, f32[8,192,16,1]{1,2,0,3:T(8,128)S(1)}, f32[8,192,16,1,128]{4,1,2,0,3:T(8,128)}, s32[]{:T(128...) while((s32[]{:T(128)}, f32[8,192,16,1]{1,2,0,3:T(8,128)S(1)}, ...), condition=%wide.region_10.11_spmd.clone, body=%wide.region_7.10_spmd.clone.sunk | while | flops 2474522624 | bytes 153828352 | solution.py:52
  678.5 12.1 constant_dynamic-slice_fusion.5
  690.6 17.0 %fusion.154 = (f32[8,192,16]{1,2,0:T(8,128)S(1)}, f32[8,16,192,192]{3,2,1,0:T(8,128)}) fusion(pred[8,192,192]{1,2,0:T(8,128)(4,1)S(1)} %broadcast_and_fusion.2, bf16[8,192,16,1,128]{4,1,2,0,3:T(8,128)(2,1)} %get-tuple-element.295, bf16[1,8,192,16,128]{4,3,2,1,0:T(8,128)(2,1)} %get-tuple-element.254), kind=kOutput, calls=%fused_computation.5.clone.1 | convolution fusion | flops 1222090752 | bytes 31850496 | tf_op jit(solution)/shard_map/while/body/bqhgd,bkhd->bqhgk/dot_general | solution.py:40
  707.6 12.1 fusion.156
  719.9 19.8 %bitcast_add_fusion.5 = f32[8,192,16,1,128]{4,1,2,0,3:T(8,128)} fusion(f32[8,192,16,1,128]{4,1,2,0,3:T(8,128)} %get-tuple-element.277, f32[8,192,16]{1,2,0:T(8,128)S(1)} %get-tuple-element.258, f32[8,16,192,192]{3,2,1,0:T(8,128)} %get-tuple-element.257, f32[8,192,16]{1,2,0:T(8,128)S(1)} %bitcast.228, ...), kind=kOutput, calls=%fused_computation.8.clone.1 | convolution fusion | flops 1233125376 | bytes 50823168 | tf_op jit(solution)/shard_map/while/body/bqhgk,bkhd->bqhgd/dot_general | solution.py:47
  739.7 8.1 divide_convert_fusion
  754.7 10.3 convert_element_type.149
  773.6 21.1 %fusion.32 = (f32[8,192]{1,0:T(8,128)S(1)}, bf16[8,192,2048]{2,1,0:T(8,128)(2,1)}) fusion(bf16[8,192,2048]{2,1,0:T(8,128)(2,1)} %convert_element_type.149, bf16[1,2048,2048]{2,1,0:T(8,128)(2,1)} %all-gather.27.cloned.1.call-done, bf16[8,192,2048]{2,1,0:T(8,128)(2,1)} %param.14), kind=kOutput, calls=%fused_computation.48 | convolution fusion | flops 12903774208 | bytes 27269120 | tf_op jit(solution)/shard_map/dot_general | solution.py:129
  808.5 34.9 %all-gather.29.cloned.1.call-done = bf16[1,2048,8192]{2,1,0:T(8,128)(2,1)} async-done(((bf16[1,2048,1024]{2,1,0:T(8,128)(2,1)}), bf16[1,2048,8192]{2,1,0:T(8,128)(2,1)}) %all-gather.29.cloned.1.call-update) | async-done | bytes 33554448 | tf_op jit(solution)/shard_map/all_gather | solution.py:119
  843.5 60.6 %fusion.24 = f32[1536,8192]{1,0:T(8,128)} fusion(bf16[1536,2048]{1,0:T(8,128)(2,1)} %bitcast.245, bf16[1,2048,8192]{2,1,0:T(8,128)(2,1)} %all-gather.29.cloned.1.call-done), kind=kOutput, calls=%fused_computation.36 | convolution fusion | flops 51539607552 | bytes 90177536 | tf_op jit(solution)/shard_map/dot_general | solution.py:131
  904.0 98.3 %all-gather.31.cloned.1.call-done = bf16[1,2048,8192]{2,1,0:T(8,128)(2,1)} async-done(((bf16[1,2048,1024]{2,1,0:T(8,128)(2,1)}), bf16[1,2048,8192]{2,1,0:T(8,128)(2,1)}) %all-gather.31.cloned.1.call-update) | async-done | bytes 33554448 | tf_op jit(solution)/shard_map/all_gather | solution.py:120
  1002.4 66.9 %multiply_convert_fusion.clone.4 = bf16[1536,8192]{1,0:T(8,128)(2,1)} fusion(f32[1536,8192]{1,0:T(8,128)} %fusion.24, bf16[1536,2048]{1,0:T(8,128)(2,1)} %bitcast.246, bf16[1,2048,8192]{2,1,0:T(8,128)(2,1)} %all-gather.31.cloned.1.call-done), kind=kOutput, calls=%fused_computation.32.clone.clone.clone.1 | convolution fusion | flops 51615105024 | bytes 115343360 | tf_op jit(solution)/shard_map/dot_general | solution.py:131
  1069.2 92.0 %all-gather.33.cloned.1.call-done = bf16[1,8192,2048]{2,1,0:T(8,128)(2,1)} async-done(((bf16[1,1024,2048]{2,1,0:T(8,128)(2,1)}), bf16[1,8192,2048]{2,1,0:T(8,128)(2,1)}) %all-gather.33.cloned.1.call-update) | async-done | bytes 33554448 | tf_op jit(solution)/shard_map/all_gather | solution.py:121
  1161.3 60.9 %fusion.21 = f32[1536,2048]{1,0:T(8,128)} fusion(bf16[1,8192,2048]{2,1,0:T(8,128)(2,1)} %all-gather.33.cloned.1.call-done, bf16[1536,8192]{1,0:T(8,128)(2,1)} %multiply_convert_fusion.clone.4), kind=kOutput, calls=%fused_computation.33 | convolution fusion | flops 51539607552 | bytes 71303168 | tf_op jit(solution)/shard_map/dot_general | solution.py:132
  1231.3 28.6 %copy.78 = bf16[1,8,1537,2,128]{4,3,2,1,0:T(2,128)(2,1)} copy(bf16[1,8,1537,2,128]{4,2,3,1,0:T(8,128)(2,1)S(1)} %copy-done.1) | data formatting | bytes 12591104
  1260.0 28.7 %copy.79 = bf16[1,8,1537,2,128]{4,3,2,1,0:T(2,128)(2,1)} copy(bf16[1,8,1537,2,128]{4,2,3,1,0:T(8,128)(2,1)S(1)} %fusion.61) | data formatting | bytes 12591104
  1297.9 231.3 %psum.23 = bf16[8,2048]{1,0:T(8,128)(2,1)} all-reduce(f32[8,2048]{1,0:T(8,128)S(1)} %bitcast.251), channel_id=1, replica_groups=mesh['replica'=2,'model'=8] {'model'}, use_global_device_ids=true, to_apply=%region_12.13 | all-reduce | flops 16384 | bytes 98304 | tf_op jit(solution)/shard_map/psum | solution.py:140
  1529.1 21.1 %all-reduce.5.cloned.1.call-done = f32[8,2048]{1,0:T(8,128)} async-done(((f32[8,2048]{1,0:T(8,128)}), f32[8,2048]{1,0:T(8,128)}) %all-reduce.5.cloned.1.call-update) | async-done | bytes 65552 | tf_op jit(solution)/shard_map/psum | solution.py:86
  (135 shorter events, 103.1 us)
Async XLA Ops:
  7.2 57.3 %all-gather.23.cloned.1.call-start = ((), (), s32[]{:S(2)}) async-start(), calls=%async_computation.5 | async-start | bytes 9437184 | tf_op jit(solution)/shard_map/all_gather | solution.py:117
  7.9 110.2 %all-gather.25.cloned.1.call-start = ((), (), s32[]{:S(2)}) async-start(), calls=%async_computation.6 | async-start | bytes 9437184 | tf_op jit(solution)/shard_map/all_gather | solution.py:115
  8.6 163.1 %all-gather.21.cloned.1.call-start = ((), (), s32[]{:S(2)}) async-start(), calls=%async_computation.4 | async-start | bytes 9437184 | tf_op jit(solution)/shard_map/all_gather | solution.py:116
  9.4 393.1 %all-gather.19.cloned.1.call-start = ((), (), s32[]{:S(2)}) async-start(), calls=%async_computation.1 | async-start | bytes 56623104 | tf_op jit(solution)/shard_map/all_gather | solution.py:127
  9.4 5.1 copy-start.2
  86.9 545.8 %all-gather.17.cloned.1.call-start = ((), (), s32[]{:S(2)}) async-start(), calls=%async_computation | async-start | bytes 56623104 | tf_op jit(solution)/shard_map/all_gather | solution.py:126
  171.7 32.1 %slice-start.2 = ((s8[6291456]{0:T(1024)(128)(4,1)}), s8[2097152]{0:T(1024)(128)(4,1)S(1)}, s32[]{:S(2)}) async-start(s8[6291456]{0:T(1024)(128)(4,1)} %bitcast.243), calls=%async_computation.13 | async-start | bytes 4194304
  184.2 19.6 %copy-start.5 = (bf16[2048,2048]{1,0:T(8,128)(2,1)S(1)}, bf16[2048,2048]{1,0:T(8,128)(2,1)}, u32[]{:S(2)}) copy-start(bf16[2048,2048]{1,0:T(8,128)(2,1)} %copy.67) | copy-start | bytes 25165828
  184.2 19.6 %slice-start.3 = ((s8[6291456]{0:T(1024)(128)(4,1)}), s8[4194304]{0:T(1024)(128)(4,1)S(1)}, s32[]{:S(2)}) async-start(s8[6291456]{0:T(1024)(128)(4,1)} %bitcast.243), calls=%async_computation.14 | async-start | bytes 8388608
  261.2 5.4 copy-start.8
  261.2 512.5 %all-gather.27.cloned.1.call-start = ((), (), s32[]{:S(2)}) async-start(), calls=%async_computation.7 | async-start | bytes 9437184 | tf_op jit(solution)/shard_map/all_gather | solution.py:118
  261.8 5.5 copy-start.18
  261.8 581.7 %all-gather.29.cloned.1.call-start = ((), (), s32[]{:S(2)}) async-start(), calls=%async_computation.8 | async-start | bytes 37748736 | tf_op jit(solution)/shard_map/all_gather | solution.py:119
  262.5 7.6 copy-start.20
  262.5 739.8 %all-gather.31.cloned.1.call-start = ((), (), s32[]{:S(2)}) async-start(), calls=%async_computation.9 | async-start | bytes 37748736 | tf_op jit(solution)/shard_map/all_gather | solution.py:120
  263.3 898.0 %all-gather.33.cloned.1.call-start = ((), (), s32[]{:S(2)}) async-start(), calls=%async_computation.10 | async-start | bytes 37748736 | tf_op jit(solution)/shard_map/all_gather | solution.py:121
  264.0 1024.6 %all-reduce.3.cloned.1.call-start = ((), (), s32[]{:S(2)}) async-start(), calls=%async_computation.2 | async-start | bytes 131072 | tf_op jit(solution)/shard_map/psum | solution.py:82
  660.1 7.2 slice-start
  660.1 7.2 slice-start.1
  707.6 12.3 copy-start
  754.7 10.3 copy-start.17
  754.7 10.3 copy-start.21
  765.0 4.8 copy-start.15
  773.6 21.1 %copy-start.9 = (bf16[1,256,2048]{2,1,0:T(8,128)(2,1)S(1)}, bf16[1,256,2048]{2,1,0:T(8,128)(2,1)}, u32[]{:S(2)}) copy-start(bf16[1,256,2048]{2,1,0:T(8,128)(2,1)} %param.21) | copy-start | bytes 3145732
  794.7 6.8 copy-start.12
  801.5 748.7 %all-reduce.5.cloned.1.call-start = ((), (), s32[]{:S(2)}) async-start(), calls=%async_computation.3 | async-start | bytes 131072 | tf_op jit(solution)/shard_map/psum | solution.py:86
  1069.2 152.9 %copy-start.14 = (pred[8,192,1]{1,0,2:T(8,128)(4,1)S(1)}, pred[8,192,1]{1,0,2:T(8,128)(4,1)}, u32[]{:S(2)}) copy-start(pred[8,192,1]{1,0,2:T(8,128)(4,1)} %compare_bitcast_fusion) | copy-start | bytes 4612
  1161.3 60.9 %copy-start.4 = (bf16[8,192,2048]{2,1,0:T(8,128)(2,1)S(1)}, bf16[8,192,2048]{2,1,0:T(8,128)(2,1)}, u32[]{:S(2)}) copy-start(bf16[8,192,2048]{2,1,0:T(8,128)(2,1)} %get-tuple-element.179) | copy-start | bytes 18874372
  1222.2 6.4 copy-start.3
  1222.2 6.4 copy-start.16
  1260.0 28.7 %copy-start.11 = (bf16[8,2048]{1,0:T(8,128)(2,1)S(1)}, bf16[8,2048]{1,0:T(8,128)(2,1)}, u32[]{:S(2)}) copy-start(bf16[8,2048]{1,0:T(8,128)(2,1)} %param.16) | copy-start | bytes 98308
  1260.0 29.7 %copy-start.13 = (f32[1,2048]{1,0:T(1,128)S(1)}, f32[1,2048]{1,0:T(1,128)}, u32[]{:S(2)}) copy-start(f32[1,2048]{1,0:T(1,128)} %mul.362) | copy-start | bytes 24580
  (5 other events, 17.3 us)
Sparse Core Ops, SparseCore 0:
  9.8 54.5 all-gather.22
  66.3 51.7 all-gather.24
  119.9 51.7 all-gather.20
  174.0 228.4 all-gather.18
  404.2 228.4 all-gather.16
  634.4 50.1 all-gather.26
  686.4 157.0 all-gather.28
  845.3 157.0 all-gather.30
  1004.2 157.0 all-gather.32
  1164.2 114.8 all-reduce.2
  1298.0 252.1 all-reduce.4
where the time goes:
time: 1570 us; the launch traced here: 1560 us
  waiting for transfers between devices  719 us (46%)
  matrix products  325 us (21%)
  blocking collectives  231 us (15%)
  local copies, waits for them, and re-layouts  174 us (11%)
  other arithmetic  94 us (6%)
    psum x1, blocking collectives, per_device(): last_hidden = lax.psum(last_part, 'model').astype(jnp.bfloat16)  231 us
    all_gather x1, waiting for transfers between devices, per_device(): key_blocks = lax.all_gather(k_rot, 'model', axis=0)  230 us
    all_gather x1, waiting for transfers between devices, per_device(): val_blocks = lax.all_gather(v_proj, 'model', axis=0)  120 us
    all_gather x1, waiting for transfers between devices, per_device(): wu_full = lax.all_gather(w_up[layer_idx], 'model', axis=1, tiled=True)  98.3 us
    all_gather x1, waiting for transfers between devices, per_device(): wd_full = lax.all_gather(w_down[layer_idx], 'model', axis=0, tiled=True)  92 us
    unnamed x55, local copies, waits for them, and re-layouts  76.5 us
    dot_general x1, matrix products, per_device(): jnp.dot(normed, wu_full, preferred_element_type=jnp.float32)  66.9 us
    dot_general x1, matrix products, per_device(): jnp.dot(mlp_mid, wd_full, preferred_element_type=jnp.float32)  60.9 us
  transfers between devices with their start and end apart: 11, of which 9 were waited for; matrix products, arithmetic and copies ran while one was open for 37% of the time, Pallas kernels for 0%

commit v1 on v0

v1 whole, which is shorter than its diff:
```python
import jax
import jax.numpy as jnp
from jax import lax
from jax.experimental import pallas as pl
from jax.experimental.pallas import tpu as pltpu
from jax.sharding import PartitionSpec as P

HEAD_DIM = 128
NEG_BIG = -1e30
BATCH = 8
SEQ_LOC = 192
D_MODEL = 2048
SHARD = 256
ROWS = 2 * SEQ_LOC
MESH = pl.DeviceIdType.MESH


def rms_norm(hidden, gain_vec):
    hid_f32 = hidden.astype(jnp.float32)
    inv_rms = lax.rsqrt(jnp.mean(hid_f32 * hid_f32, axis=-1, keepdims=True) + 1e-5)
    return (hid_f32 * inv_rms * gain_vec.astype(jnp.float32)).astype(jnp.bfloat16)


def rope_tables(positions):
    half_dim = HEAD_DIM // 2
    inv_freq = 10000.0 ** (-2.0 * jnp.arange(half_dim, dtype=jnp.float32) / HEAD_DIM)
    angles = positions.astype(jnp.float32)[..., None] * inv_freq
    cos_tab, sin_tab = jnp.cos(angles), jnp.sin(angles)
    return jnp.concatenate([cos_tab, cos_tab], -1), jnp.concatenate([-sin_tab, sin_tab], -1)


def rotary(heads_f32, positions):
    cos_tab, sin_tab = rope_tables(positions)
    half_dim = HEAD_DIM // 2
    swapped = jnp.concatenate([heads_f32[..., half_dim:], heads_f32[..., :half_dim]], axis=-1)
    return heads_f32 * cos_tab[..., None, :] + swapped * sin_tab[..., None, :]


def kv_kernel(prompt, gain, tabc, tabs, wk, wv, kv_out, xbuf, xrecv, wbuf, tmp, stage,
              lsem, xsem, ysend, yrecv, wsend, wrecv, osend, orecv, ssem):
    rep = lax.axis_index('replica')
    me = lax.axis_index('model')
    core = lax.rem(me, 2)
    xpos = lax.rem(me // 2, 2)
    ypos = me // 4
    sib = me + 1 - 2 * core
    xnb = me + 2 - 4 * xpos
    xsb = xnb + 1 - 2 * core
    ynb = me + 4 - 8 * ypos
    znb = 1 - rep

    barrier = pltpu.get_barrier_semaphore()
    for peer in ((rep, sib), (rep, xnb), (rep, xsb), (rep, ynb), (znb, me)):
        pl.semaphore_signal(barrier, inc=1, device_id=peer, device_id_type=MESH)
    pl.semaphore_wait(barrier, 5)

    def remote(src, dst, send, recv, peer):
        return pltpu.make_async_remote_copy(src_ref=src, dst_ref=dst, send_sem=send, recv_sem=recv, device_id=peer, device_id_type=MESH)

    def y_copy(b):
        return remote(prompt.at[b], xrecv.at[b], ysend.at[b], yrecv.at[b], (rep, ynb))

    def x_load(b):
        return pltpu.make_async_copy(prompt.at[b], xbuf.at[b], xsem.at[b])

    wk_load = pltpu.make_async_copy(wk, wbuf.at[0, 0], lsem.at[0])
    wv_load = pltpu.make_async_copy(wv, wbuf.at[0, 1], lsem.at[1])
    wk_load.start()
    wv_load.start()

    @pl.loop(0, BATCH)
    def _(b):
        y_copy(b).start()
        x_load(b).start()

    wk_load.wait()
    wv_load.wait()
    w_x = remote(wbuf.at[0, rep], wbuf.at[2, rep], wsend.at[0], wrecv.at[0], (rep, xnb))
    w_s = remote(wbuf.at[0], wbuf.at[1], wsend.at[1], wrecv.at[1], (rep, sib))
    w_z = remote(wbuf.at[2, rep], wbuf.at[2, rep], wsend.at[2], wrecv.at[2], (znb, me))
    w_xs = remote(wbuf.at[2, rep], wbuf.at[3, rep], wsend.at[3], wrecv.at[3], (rep, sib))
    w_zs = remote(wbuf.at[2, znb], wbuf.at[3, znb], wsend.at[4], wrecv.at[4], (rep, sib))
    w_x.start()
    w_s.start()

    def out_copy(s, b, o, kv):
        blk = me if s == 0 else ynb
        dst = kv_out.at[kv, b, pl.ds(pl.multiple_of(blk * ROWS, ROWS), ROWS), :]
        src = stage.at[s, b, o, kv]
        if o == 0:
            return pltpu.make_async_copy(src, dst, ssem.at[s, b, kv])
        peer = (sib, xnb, xsb)[o - 1]
        return remote(src, dst, osend.at[o - 1, s, b, kv], orecv.at[o - 1, s, b, kv], (rep, peer))

    def normalize(buf, b):
        x = buf[b].astype(jnp.float32)
        inv = lax.rsqrt(jnp.mean(x * x, axis=-1, keepdims=True) + 1e-5)
        buf[b] = (x * inv * gain[...].astype(jnp.float32)).astype(jnp.bfloat16)

    def project(buf, s, b, o, kv):
        acc = jnp.dot(buf[b], wbuf[o, kv], preferred_element_type=jnp.float32)
        c, sn = tabc[kv, s], tabs[kv, s]
        for h in range(2):
            a = acc[:, h * HEAD_DIM:(h + 1) * HEAD_DIM]
            tmp[pl.ds(h, SEQ_LOC, stride=2), :] = a * c + pltpu.roll(a, HEAD_DIM // 2, 1) * sn
        stage[s, b, o, kv] = tmp[...].astype(jnp.bfloat16)

    @pl.loop(0, BATCH)
    def _(b):
        x_load(b).wait()
        normalize(xbuf, b)

        @pl.loop(0, 2)
        def _(kv):
            project(xbuf, 0, b, 0, kv)
            out_copy(0, b, 0, kv).start()

    w_s.wait_recv()

    @pl.loop(0, BATCH)
    def _(b):
        @pl.loop(0, 2)
        def _(kv):
            project(xbuf, 0, b, 1, kv)
            out_copy(0, b, 1, kv).start()

    w_x.wait_recv()
    w_z.start()
    w_xs.start()
    w_xs.wait_recv()

    def own_x_phase(kv):
        @pl.loop(0, BATCH)
        def _(b):
            for o in (2, 3):
                project(xbuf, 0, b, o, kv)
            for o in (2, 3):
                out_copy(0, b, o, kv).start()

    own_x_phase(rep)
    w_z.wait_recv()
    w_zs.start()
    w_zs.wait_recv()
    own_x_phase(znb)

    @pl.loop(0, BATCH)
    def _(b):
        y_copy(b).wait_recv()
        normalize(xrecv, b)

        @pl.loop(0, 2)
        def _(kv):
            for o in (2, 3, 1, 0):
                project(xrecv, 1, b, o, kv)
                out_copy(1, b, o, kv).start()

    for w in (w_x, w_s, w_z, w_xs, w_zs):
        w.wait_send()

    @pl.loop(0, BATCH)
    def _(b):
        y_copy(b).wait_send()
        for s in range(2):
            for kv in range(2):
                out_copy(s, b, 0, kv).wait()
                for o in (1, 2, 3):
                    out_copy(s, b, o, kv).wait()


def prompt_kv(prompt, gain, tabc, tabs, wk, wv):
    vmem = pl.BlockSpec(memory_space=pltpu.VMEM)
    anym = pl.BlockSpec(memory_space=pl.ANY)
    dma = pltpu.SemaphoreType.DMA
    bf = jnp.bfloat16
    return pl.pallas_call(
        kv_kernel,
        out_shape=jax.ShapeDtypeStruct((2, BATCH, 8 * ROWS, HEAD_DIM), bf),
        in_specs=[anym, vmem, vmem, vmem, anym, anym],
        out_specs=anym,
        scratch_shapes=[
            pltpu.VMEM((BATCH, SEQ_LOC, D_MODEL), bf),
            pltpu.VMEM((BATCH, SEQ_LOC, D_MODEL), bf),
            pltpu.VMEM((4, 2, D_MODEL, SHARD), bf),
            pltpu.VMEM((ROWS, HEAD_DIM), jnp.float32),
            pltpu.VMEM((2, BATCH, 4, 2, ROWS, HEAD_DIM), bf),
            dma((2,)), dma((BATCH,)), dma((BATCH,)), dma((BATCH,)), dma((5,)), dma((5,)),
            dma((3, 2, BATCH, 2)), dma((3, 2, BATCH, 2)), dma((2, BATCH, 2)),
        ],
        compiler_params=pltpu.CompilerParams(collective_id=0, has_side_effects=True, vmem_limit_bytes=56 * 1024 * 1024),
        cost_estimate=pl.CostEstimate(flops=26_000_000_000, bytes_accessed=40_000_000, transcendentals=0),
        name='prompt_kv',
    )(prompt, gain, tabc, tabs, wk, wv)


def solution(mesh):
    seq_spec = P('replica', 'model', None)
    col_spec = P(None, None, 'model')
    row_spec = P(None, 'model', None)
    gain_spec = P(None, None)
    tok_spec = P('replica', None)
    cache_spec = P(None, 'replica', None, 'model', None)
    in_specs = (seq_spec, P('replica'), tok_spec, gain_spec, col_spec, col_spec, col_spec, row_spec, gain_spec, col_spec, col_spec, row_spec)
    out_specs = (tok_spec, tok_spec, cache_spec, cache_spec)

    def per_device(prompt, lengths, new_tok, norm_attn, w_q, w_k, w_v, w_o, norm_mlp, w_gate, w_up, w_down):
        f32, bf = jnp.float32, jnp.bfloat16
        me = lax.axis_index('model')
        n_batch, seq_loc, d_model = prompt.shape
        seq_len = seq_loc * mesh.shape['model']
        pos = jnp.stack([me * seq_loc, lax.rem(me + 4, 8) * seq_loc])[:, None] + jnp.arange(seq_loc)[None, :]
        cos_k, sin_k = rope_tables(pos)
        tabc = jnp.stack([cos_k, jnp.ones_like(cos_k)])
        tabs = jnp.stack([sin_k, jnp.zeros_like(sin_k)])
        kv = prompt_kv(prompt, norm_attn, tabc, tabs, w_k[0], w_v[0]).reshape(2, n_batch, seq_len, 2, HEAD_DIM)

        seq_pos = me * seq_loc + jnp.arange(seq_loc)
        last_sel = (seq_pos[None, :] == (lengths - 1)[:, None]).astype(bf)
        last_part = jnp.einsum('bs,bsd->bd', last_sel, prompt, preferred_element_type=f32)
        last_row = lax.psum(last_part, 'model').astype(bf)
        rows = jnp.concatenate([new_tok, last_row], axis=0)
        row_pos = jnp.concatenate([lengths, lengths - 1])
        normed = rms_norm(rows, norm_attn[0])
        q = rotary(jnp.dot(normed, w_q[0], preferred_element_type=f32).reshape(2 * n_batch, 2, HEAD_DIM), row_pos).astype(bf)
        k_new = rotary(jnp.dot(normed[:n_batch], w_k[0], preferred_element_type=f32).reshape(n_batch, 2, HEAD_DIM), lengths).astype(bf)
        v_new = jnp.dot(normed[:n_batch], w_v[0], preferred_element_type=f32).astype(bf).reshape(n_batch, 2, HEAD_DIM)

        q2 = jnp.moveaxis(q.reshape(2, n_batch, 2, HEAD_DIM), 0, 1)
        scores = jnp.einsum('bghd,bkhd->bghk', q2, kv[0], preferred_element_type=f32) * (HEAD_DIM ** -0.5)
        visible = jnp.arange(seq_len)[None, :] < lengths[:, None]
        scores = jnp.where(visible[:, None, None, :], scores, NEG_BIG)
        self_score = jnp.sum(q2[:, 0].astype(f32) * k_new.astype(f32), axis=-1) * (HEAD_DIM ** -0.5)
        self_score = jnp.stack([self_score, jnp.full_like(self_score, NEG_BIG)], axis=1)
        top = jnp.maximum(jnp.max(scores, axis=-1), self_score)
        prob = jnp.exp(scores - top[..., None])
        self_prob = jnp.exp(self_score - top)
        acc = jnp.einsum('bghk,bkhd->bghd', prob.astype(bf), kv[1], preferred_element_type=f32)
        acc = acc + self_prob[..., None] * v_new.astype(f32)[:, None]
        attn = (acc / (jnp.sum(prob, axis=-1) + self_prob)[..., None]).astype(bf)
        attn = jnp.moveaxis(attn, 1, 0).reshape(2 * n_batch, 2 * HEAD_DIM)
        attn_part = jnp.dot(attn, w_o[0], preferred_element_type=f32)
        hid = (rows.astype(f32) + lax.psum(attn_part, 'model')).astype(bf)
        normed = rms_norm(hid, norm_mlp[0])
        mid = (jax.nn.silu(jnp.dot(normed, w_gate[0], preferred_element_type=f32)) * jnp.dot(normed, w_up[0], preferred_element_type=f32)).astype(bf)
        mlp_part = jnp.dot(mid, w_down[0], preferred_element_type=f32)
        hid = (hid.astype(f32) + lax.psum(mlp_part, 'model')).astype(bf)

        key_cache = jnp.concatenate([kv[0], k_new[:, None]], axis=1)[None]
        val_cache = jnp.concatenate([kv[1], v_new[:, None]], axis=1)[None]
        return hid[:n_batch], hid[n_batch:], key_cache, val_cache

    return jax.shard_map(per_device, mesh=mesh, in_specs=in_specs, out_specs=out_specs, check_vma=False)
```

time: 1570 us -> 346 us (0.22)
  waiting for transfers between devices: 719 us -> 57 us
  matrix products: 325 us -> 21 us
  blocking collectives: 231 us -> 23.1 us
  Pallas kernels: 0 us -> 172 us
  local copies, waits for them, and re-layouts: 174 us -> 17 us
  other arithmetic: 94 us -> 40.4 us
    all_gather x9 -> x0, waiting for transfers between devices: 693 us -> none  [the longest x1 230 us: per_device(): key_blocks = lax.all_gather(k_rot, 'model', axis=0)]
    dot_general x18 -> x9, matrix products: 325 us -> 21 us  [the longest x1 5.39 us: per_device(): mlp_part = jnp.dot(mid, w_down[0], preferred_element_type=f32)]
    psum x1, blocking collectives: 231 us -> 23.1 us  [per_device(): last_row = lax.psum(last_part, 'model').astype(bf)]
    pallas_call x0 -> x1, Pallas kernels: none -> 172 us  [prompt_kv(): pl.pallas_call(kv_kernel, out_shape=jax.ShapeDtypeStruct((2, BATCH, 8 * R...]
    unnamed x55 -> x16, local copies, waits for them, and re-layouts: 76.5 us -> 0.05 us
    concatenate x5 -> x2, other arithmetic: 45.3 us -> 0.15 us  [rope_tables(): jnp.concatenate([cos_tab, cos_tab], -1)]
    dynamic_slice x2 -> x0, local copies, waits for them, and re-layouts: 39.6 us -> none  [the longest x1 27.5 us: per_device(): lax.dynamic_slice_in_dim(val_blocks, my_idx * kv_loc, kv_loc, axis=3)]
    psum x2, waiting for transfers between devices: 21.1 us -> 57 us  [the longest x1 28.6 us: per_device(): hid = (rows.astype(f32) + lax.psum(attn_part, 'model')).astype(bf)]
  transfers between devices with their start and end apart: 11 -> 2, of which waited for: 9 -> 2; matrix products, arithmetic and copies ran while one was open for 37% -> 10% of each run, Pallas kernels for 0% -> 0%
where the time goes in v1:
time: 346 us
  Pallas kernels  172 us (50%)
  waiting for transfers between devices  57 us (16%)
  other arithmetic  40.4 us (12%)
  blocking collectives  23.1 us (7%)
  matrix products  21 us (6%)
  local copies, waits for them, and re-layouts  17 us (5%)
  between operations  14.3 us (4%)
    pallas_call x1, Pallas kernels, prompt_kv(): pl.pallas_call(kv_kernel, out_shape=jax.ShapeDtypeStruct((2, BATCH, 8 * R...  172 us
    psum x1, waiting for transfers between devices, per_device(): hid = (rows.astype(f32) + lax.psum(attn_part, 'model')).astype(bf)  28.6 us
    psum x1, waiting for transfers between devices, per_device(): hid = (hid.astype(f32) + lax.psum(mlp_part, 'model')).astype(bf)  28.4 us
    psum x1, blocking collectives, per_device(): last_row = lax.psum(last_part, 'model').astype(bf)  23.1 us
    broadcast_in_dim x1, other arithmetic, per_device(): key_cache = jnp.concatenate([kv[0], k_new[:, None]], axis=1)[None]  16.9 us
    broadcast_in_dim x1, other arithmetic, per_device(): val_cache = jnp.concatenate([kv[1], v_new[:, None]], axis=1)[None]  16.9 us
    slice x1, local copies, waits for them, and re-layouts, per_device(): kv[0]  11.4 us
  transfers between devices with their start and end apart: 2, of which 2 were waited for; matrix products, arithmetic and copies ran while one was open for 10% of the time, Pallas kernels for 0%

profile of v1, /device:TPU:0, one launch (start us, length us, event | category | flops | bytes accessed | tf_op | source)
XLA Modules:
  0.0 345.5 jit_solution(12018969508049022763)
XLA Ops:
  7.2 0.8 fusion.90
  8.0 0.7 iota_compare_fusion
  8.9 0.7 mul.221
  9.6 0.8 fusion.60
  10.4 0.2 maximum_bitcast_fusion.2
  10.5 0.8 stack.29.tabc
  11.3 0.8 stack.31.tabs
  12.1 172.4 %prompt_kv.1 = bf16[2,8,3072,128]{3,2,1,0:T(8,128)(2,1)} custom-call(bf16[8,192,2048]{2,1,0:T(8,128)(2,1)} %prompt.1, bf16[1,2048]{1,0:T(2,128)(2,1)} %gain.1, f32[2,2,192,128]{3,2,1,0:T(8,128)} %stack.29.tabc, f32[2,2,192,128]{3,2,1,0:T(8,128)} %stack.31.tabs, bf16[2048,256]{1,0:T(8,128)(2,1)} %bitcast.105, bf16[2048,256]{1,0:T(8,128)(2,1)} %bitcast.104), custom_call_target="tpu_custom_call" | custom-call | flops 25999998976 | bytes 40000000 | tf_op jit(solution)/shard_map/prompt_kv/pallas_call | solution.py:175
  184.5 11.4 %fusion.86 = (bf16[1,8,3072,128]{3,2,1,0:T(8,128)(2,1)}, bf16[1,8,3072,128]{3,2,1,0:T(8,128)(2,1)}) fusion(bf16[2,8,3072,128]{3,2,1,0:T(8,128)(2,1)} %prompt_kv.1), kind=kLoop, calls=%fused_computation.104 | loop fusion | bytes 25165824 | tf_op jit(solution)/shard_map/slice | solution.py:228
  196.0 0.6 copy.54
  196.8 3.8 %fusion.64 = f32[8,1,2048]{2,1,0:T(1,128)S(1)} fusion(bf16[8,192,2048]{2,1,0:T(8,128)(2,1)} %prompt.1, pred[8,192,1]{1,0,2:T(8,128)(4,1)S(1)} %compare_bitcast_fusion), kind=kOutput, calls=%fused_computation.60 | convolution fusion | flops 6291456 | bytes 6358528 | tf_op jit(solution)/shard_map/bs,bsd->bd/dot_general | solution.py:218
  200.6 23.1 %psum.21 = bf16[8,2048]{1,0:T(8,128)(2,1)S(1)} all-reduce(f32[8,2048]{1,0:T(8,128)S(1)} %bitcast.107), channel_id=1, replica_groups=mesh['replica'=2,'model'=8] {'model'}, use_global_device_ids=true, to_apply=%region_0.0 | all-reduce | flops 16384 | bytes 98304 | tf_op jit(solution)/shard_map/psum | solution.py:219
  223.7 0.1 fusion.41
  224.0 0.2 bitcast_convert_fusion
  224.2 0.4 fusion.53
  225.1 2.4 copy.56
  227.5 1.6 fusion.61
  229.3 0.2 fusion.75
  229.5 4.8 %fusion.91 = (f32[8,2,2]{1,2,0:T(2,128)S(1)}, f32[8,2,2,1536]{3,1,2,0:T(2,128)S(1)}) fusion(bf16[8,2,2,128]{3,0,1,2:T(8,128)(2,1)S(1)} %bitcast.110, bf16[8,1536,2,128]{3,2,1,0:T(2,128)(2,1)} %bitcast.99, pred[8,1536]{1,0:T(8,128)(4,1)S(1)} %iota_compare_fusion), kind=kOutput, calls=%fused_computation.109 | convolution fusion | flops 12730336 | bytes 6508672 | tf_op jit(solution)/shard_map/bghd,bkhd->bghk/dot_general | solution.py:228
  234.3 0.3 fusion.49
  234.7 1.0 fusion.34
  235.7 0.9 fusion.37
  236.7 0.2 all-reduce.8.cloned.1.call-start
  236.9 16.9 %maximum_bitcast_fusion = bf16[1,8,1537,2,128]{4,3,2,1,0:T(2,128)(2,1)} fusion(bf16[8,1,2,128]{3,2,1,0:T(2,128)(2,1)S(1)} %copy.50, bf16[8,1536,2,128]{3,2,1,0:T(2,128)(2,1)} %bitcast.100), kind=kLoop, calls=%fused_computation | loop fusion | flops 3147776 | bytes 12591104 | tf_op jit(solution)/shard_map/broadcast_in_dim | solution.py:247
  253.9 28.6 %all-reduce.6.cloned.1.call-done = f32[16,2048]{1,0:T(8,128)} async-done(((f32[16,2048]{1,0:T(8,128)}), f32[16,2048]{1,0:T(8,128)}) %all-reduce.6.cloned.1.call-update) | async-done | bytes 131088 | tf_op jit(solution)/shard_map/psum | solution.py:241
  282.5 1.0 fusion.45
  283.5 2.9 fusion.8
  286.4 5.4 %fusion.4 = f32[16,2048]{1,0:T(8,128)} fusion(bf16[1,1024,2048]{2,1,0:T(8,128)(2,1)} %param.23, bf16[1,2048,1024]{2,1,0:T(8,128)(2,1)} %param.22, f32[16,1024]{1,0:T(8,128)S(1)} %fusion.8, bf16[16,2048]{1,0:T(8,128)(2,1)S(1)} %get-tuple-element.5, f32[2048]{0:T(1024)S(1)} %bitcast.109, f32[16]{0:T(128)S(1)} %add_rsqrt_fusion), kind=kOutput, calls=%fused_computation.6 | convolution fusion | flops 134447104 | bytes 8659008 | tf_op jit(solution)/shard_map/dot_general | solution.py:244
  291.8 16.9 %maximum_bitcast_fusion.1 = bf16[1,8,1537,2,128]{4,3,2,1,0:T(2,128)(2,1)} fusion(bf16[8,1,2,128]{3,2,1,0:T(2,128)(2,1)S(1)} %copy.51, bf16[8,1536,2,128]{3,2,1,0:T(2,128)(2,1)} %bitcast.95), kind=kLoop, calls=%fused_computation.1 | loop fusion | flops 3147776 | bytes 12591104 | tf_op jit(solution)/shard_map/broadcast_in_dim | solution.py:248
  308.7 28.4 %all-reduce.8.cloned.1.call-done = f32[16,2048]{1,0:T(8,128)} async-done(((f32[16,2048]{1,0:T(8,128)}), f32[16,2048]{1,0:T(8,128)}) %all-reduce.8.cloned.1.call-update) | async-done | bytes 131088 | tf_op jit(solution)/shard_map/psum | solution.py:245
  337.1 0.9 fusion.48
  338.1 0.6 fusion.87
  (46 shorter events, 1.4 us)
Async XLA Ops:
  7.2 228.6 %copy-start = (bf16[1,256,2048]{2,1,0:T(8,128)(2,1)S(1)}, bf16[1,256,2048]{2,1,0:T(8,128)(2,1)}, u32[]{:S(2)}) copy-start(bf16[1,256,2048]{2,1,0:T(8,128)(2,1)} %param.19) | copy-start | bytes 3145732
  7.2 275.3 %all-reduce.6.cloned.1.call-start = ((), (), s32[]{:S(2)}) async-start(), calls=%async_computation | async-start | bytes 262144 | tf_op jit(solution)/shard_map/psum | solution.py:241
  184.5 11.5 %copy-start.1 = (bf16[1,2048,256]{2,1,0:T(8,128)(2,1)S(1)}, bf16[1,2048,256]{2,1,0:T(8,128)(2,1)}, u32[]{:S(2)}) copy-start(bf16[1,2048,256]{2,1,0:T(8,128)(2,1)} %param.16) | copy-start | bytes 3145732
  184.5 12.1 %copy-start.5 = (s32[8]{0:T(128)S(1)}, s32[8]{0:T(128)}, u32[]{:S(2)}) copy-start(s32[8]{0:T(128)} %param.13) | copy-start | bytes 100
  196.0 27.8 %copy-start.3 = (bf16[8,2048]{1,0:T(8,128)(2,1)S(1)}, bf16[8,2048]{1,0:T(8,128)(2,1)}, u32[]{:S(2)}) copy-start(bf16[8,2048]{1,0:T(8,128)(2,1)} %param.14) | copy-start | bytes 98308
  196.6 27.4 %copy-start.2 = (bf16[1,2048,256]{2,1,0:T(8,128)(2,1)S(1)}, bf16[1,2048,256]{2,1,0:T(8,128)(2,1)}, u32[]{:S(2)}) copy-start(bf16[1,2048,256]{2,1,0:T(8,128)(2,1)} %param.18) | copy-start | bytes 3145732
  225.1 9.6 %slice-start = ((s8[6291456]{0:T(1024)(128)(4,1)}), s8[2097152]{0:T(1024)(128)(4,1)S(1)}, s32[]{:S(2)}) async-start(s8[6291456]{0:T(1024)(128)(4,1)} %bitcast.96), calls=%async_computation.2 | async-start | bytes 4194304
  229.5 5.1 %slice-start.1 = ((s8[6291456]{0:T(1024)(128)(4,1)}), s8[4194304]{0:T(1024)(128)(4,1)S(1)}, s32[]{:S(2)}) async-start(s8[6291456]{0:T(1024)(128)(4,1)} %bitcast.96), calls=%async_computation.3 | async-start | bytes 8388608
  236.7 100.5 %all-reduce.8.cloned.1.call-start = ((), (), s32[]{:S(2)}) async-start(), calls=%async_computation.1 | async-start | bytes 262144 | tf_op jit(solution)/shard_map/psum | solution.py:245
  236.9 16.9 %copy-start.4 = (bf16[1,2048]{1,0:T(2,128)(2,1)S(1)}, bf16[1,2048]{1,0:T(2,128)(2,1)}, u32[]{:S(2)}) copy-start(bf16[1,2048]{1,0:T(2,128)(2,1)} %param.20) | copy-start | bytes 12292
Sparse Core Ops, SparseCore 0:
  236.8 45.6 all-reduce.5
  291.9 45.1 all-reduce.7

commit v2 on v1

v2 whole, which is shorter than its diff:
```python
import jax
import jax.numpy as jnp
import numpy as np
from jax import lax
from jax.experimental import pallas as pl
from jax.experimental.pallas import tpu as pltpu
from jax.sharding import PartitionSpec as P

HEAD_DIM = 128
HALF = HEAD_DIM // 2
NEG_BIG = -1e30
BATCH = 8
SEQ_LOC = 192
SEQ_LEN = 1536
D_MODEL = 2048
SHARD = 256
FF_LOC = 1024
ROWS = 2 * SEQ_LOC
TAB_ROWS = SEQ_LEN + 8
MESH = pl.DeviceIdType.MESH
BF = jnp.bfloat16
F32 = jnp.float32
SCALE = HEAD_DIM ** -0.5


def rope_table():
    inv_freq = np.float32(10000.0) ** (np.float32(-2.0) * np.arange(HALF, dtype=np.float32) / np.float32(HEAD_DIM))
    angles = np.arange(TAB_ROWS, dtype=np.float32)[:, None] * inv_freq.astype(np.float32)
    return np.concatenate([np.cos(angles), np.sin(angles)], axis=-1).astype(np.float32)


def norm_rows(x, gain):
    inv = lax.rsqrt(jnp.mean(x * x, axis=-1, keepdims=True) + 1e-5)
    return (x * inv * gain.astype(F32)).astype(BF)


def spread(tab):
    swapped = pltpu.roll(tab, HALF, 1)
    low = lax.broadcasted_iota(jnp.int32, tab.shape, 1) < HALF
    return jnp.where(low, tab, swapped), jnp.where(low, -swapped, tab)


def rotate(a, c, s):
    return a * c + pltpu.roll(a, HALF, 1) * s


def layer_kernel(lens, prompt, new_tok, gain_a, gain_m, table, wq, wk, wv, wo, wg, wu, wd,
                 kv_out, new_out, dec_out, last_out,
                 xbuf, xrecv, wbuf, wqb, wob, wgb, wub, wdb, tab, tmp, stage,
                 lastf, lsend, lrecv, rows, qall, part, precv, kself, vself, attn, flat,
                 psend, rrecv, hid, norm2,
                 lsem, xsem, ysend, yrecv, wsend, wrecv, osend, orecv, ssem,
                 l_s, l_r, q_s, q_r, p_s, p_r, r_s, r_r, a_s, a_r):
    rep = lax.axis_index('replica')
    me = lax.axis_index('model')
    core = lax.rem(me, 2)
    xpos = lax.rem(me // 2, 2)
    ypos = me // 4
    flips = (1 - 2 * core, 2 - 4 * xpos, 4 - 8 * ypos)
    near = [me + sum(f for i, f in enumerate(flips) if d >> i & 1) for d in range(8)]
    sib, xnb, xsb, ynb = near[1], near[2], near[3], near[4]
    znb = 1 - rep

    barrier = pltpu.get_barrier_semaphore()
    for peer in [(rep, near[d]) for d in range(1, 8)] + [(znb, me)]:
        pl.semaphore_signal(barrier, inc=1, device_id=peer, device_id_type=MESH)
    pl.semaphore_wait(barrier, 8)

    def remote(src, dst, send, recv, peer):
        return pltpu.make_async_remote_copy(src_ref=src, dst_ref=dst, send_sem=send, recv_sem=recv, device_id=peer, device_id_type=MESH)

    def y_copy(b):
        return remote(prompt.at[b], xrecv.at[b], ysend.at[b], yrecv.at[b], (rep, ynb))

    def x_load(b):
        return pltpu.make_async_copy(prompt.at[b], xbuf.at[b], xsem.at[b])

    loads = [pltpu.make_async_copy(a, b, lsem.at[i]) for i, (a, b) in enumerate((
        (wk.at[0], wbuf.at[0, 0]), (wv.at[0], wbuf.at[0, 1]), (table, tab), (wq.at[0], wqb), (wo.at[0], wob),
        (wg.at[0], wgb), (wu.at[0], wub), (wd.at[0], wdb)))]
    loads[0].start()
    loads[1].start()
    y_copy(0).start()

    @pl.loop(0, BATCH)
    def _(b):
        x_load(b).start()

    for load in loads[2:]:
        load.start()
    loads[0].wait()
    loads[1].wait()
    w_x = remote(wbuf.at[0, rep], wbuf.at[2, rep], wsend.at[0], wrecv.at[0], (rep, xnb))
    w_s = remote(wbuf.at[0], wbuf.at[1], wsend.at[1], wrecv.at[1], (rep, sib))
    w_z = remote(wbuf.at[2, rep], wbuf.at[2, rep], wsend.at[2], wrecv.at[2], (znb, me))
    w_xs = remote(wbuf.at[2, rep], wbuf.at[3, rep], wsend.at[3], wrecv.at[3], (rep, sib))
    w_zs = remote(wbuf.at[2, znb], wbuf.at[3, znb], wsend.at[4], wrecv.at[4], (rep, sib))
    w_x.start()
    w_s.start()

    def out_copy(s, b, o, kv):
        blk = me if s == 0 else ynb
        dst = kv_out.at[kv, b, pl.ds(pl.multiple_of(blk * ROWS, ROWS), ROWS), :]
        src = stage.at[s, b, o, kv]
        if o == 0:
            return pltpu.make_async_copy(src, dst, ssem.at[s, b, kv])
        return remote(src, dst, osend.at[o - 1, s, b, kv], orecv.at[o - 1, s, b, kv], (rep, near[o]))

    def project(buf, s, b, o, kv):
        acc = jnp.dot(buf[b], wbuf[o, kv], preferred_element_type=F32)
        blk = me if s == 0 else ynb
        c, sn = spread(tab[pl.ds(pl.multiple_of(blk * SEQ_LOC, SEQ_LOC), SEQ_LOC), :])
        is_k = kv == 0
        c = jnp.where(is_k, c, 1.0)
        sn = jnp.where(is_k, sn, 0.0)
        for h in range(2):
            tmp[pl.ds(h, SEQ_LOC, stride=2), :] = rotate(acc[:, h * HEAD_DIM:(h + 1) * HEAD_DIM], c, sn)
        stage[s, b, o, kv] = tmp[...].astype(BF)

    @pl.loop(0, BATCH)
    def _(b):
        x_load(b).wait()
        x = xbuf[b].astype(F32)
        here = me * SEQ_LOC + lax.broadcasted_iota(jnp.int32, (SEQ_LOC, 1), 0) == lens[b] - 1
        lastf[pl.ds(b, 1), :] = jnp.sum(jnp.where(here, x, 0.0), axis=0, keepdims=True)
        xbuf[b] = norm_rows(x, gain_a[...])

    l_copy = [remote(lsend.at[i], lrecv.at[i], l_s.at[i], l_r.at[i], (rep, near[d])) for i, d in enumerate((4, 1, 2))]
    lsend[0] = lastf[...].astype(BF)
    loads[2].wait()
    l_copy[0].start()

    @pl.loop(1, BATCH)
    def _(b):
        y_copy(b).start()

    @pl.loop(0, BATCH)
    def _(b):
        @pl.loop(0, 2)
        def _(kv):
            project(xbuf, 0, b, 0, kv)
            out_copy(0, b, 0, kv).start()

    def join_last(i):
        l_copy[i].wait_recv()
        return (lsend[i].astype(F32) + lrecv[i].astype(F32)).astype(BF)

    lsend[1] = join_last(0)
    w_s.wait_recv()
    l_copy[1].start()

    @pl.loop(0, BATCH)
    def _(b):
        @pl.loop(0, 2)
        def _(kv):
            project(xbuf, 0, b, 1, kv)
            out_copy(0, b, 1, kv).start()

    lsend[2] = join_last(1)

    w_x.wait_recv()
    w_z.start()
    w_xs.start()
    l_copy[2].start()
    w_xs.wait_recv()

    def own_x_phase(kv):
        @pl.loop(0, BATCH)
        def _(b):
            for o in (2, 3):
                project(xbuf, 0, b, o, kv)
            for o in (2, 3):
                out_copy(0, b, o, kv).start()

    own_x_phase(rep)

    rows[0:BATCH, :] = new_tok[...].astype(F32)
    rows[BATCH:2 * BATCH, :] = join_last(2).astype(F32)
    loads[3].wait()
    n16 = norm_rows(rows[...], gain_a[...])
    q16 = jnp.dot(n16, wqb[...], preferred_element_type=F32)
    k16 = jnp.dot(n16, wbuf[0, 0], preferred_element_type=F32)
    v16 = jnp.dot(n16, wbuf[0, 1], preferred_element_type=F32)
    for b in range(BATCH):
        flat[pl.ds(b, 1), 0:HEAD_DIM] = tab[pl.ds(jnp.clip(lens[b], 0, SEQ_LEN), 1), :]
        flat[pl.ds(BATCH + b, 1), 0:HEAD_DIM] = tab[pl.ds(jnp.clip(lens[b] - 1, 0, SEQ_LEN), 1), :]
    c16, s16 = spread(flat[:, 0:HEAD_DIM])
    kself[...] = jnp.zeros_like(kself)
    vself[...] = jnp.zeros_like(vself)
    for h in range(2):
        lanes = slice(h * HEAD_DIM, (h + 1) * HEAD_DIM)
        qh = rotate(q16[:, lanes], c16, s16).astype(BF).astype(F32)
        kh = rotate(k16[:, lanes], c16, s16)[:BATCH].astype(BF).astype(F32)
        vh = v16[:BATCH, lanes].astype(BF).astype(F32)
        for g in range(2):
            qall[0, :, 2 * g + h, :] = qh[g * BATCH:(g + 1) * BATCH]
        kself[:, h, :] = kh
        vself[:, h, :] = vh
        tmp[pl.ds(h, BATCH, stride=2), :] = kh
        tmp[pl.ds(2 * BATCH + h, BATCH, stride=2), :] = vh
    new_out[0] = tmp[0:2 * BATCH, :].astype(BF)
    new_out[1] = tmp[2 * BATCH:4 * BATCH, :].astype(BF)
    low = lax.broadcasted_iota(jnp.int32, (4, HEAD_DIM), 1) < HALF
    part[:, 0] = jnp.zeros((4, BATCH, 4, HEAD_DIM), F32)
    part[:, 1] = jnp.broadcast_to(jnp.where(low, NEG_BIG, 0.0), (4, BATCH, 4, HEAD_DIM))
    q_copy = [remote(qall.at[0], qall.at[d], q_s.at[d - 1], q_r.at[d - 1], (rep, near[d])) for d in (1, 2, 3)]
    for c in q_copy:
        c.start()

    w_z.wait_recv()
    w_zs.start()
    w_zs.wait_recv()
    own_x_phase(znb)
    for c in q_copy:
        c.wait_recv()

    lane = lax.broadcasted_iota(jnp.int32, (4, ROWS), 1)
    same_head = lane % 2 == lax.broadcasted_iota(jnp.int32, (4, ROWS), 0) % 2

    def attend(s, b):
        blk = me if s == 0 else ynb
        seen = same_head & (blk * SEQ_LOC + lane // 2 < lens[b])
        for o in range(4):
            sc = lax.dot_general(qall[o, b].astype(BF), stage[s, b, o, 0], (((1,), (1,)), ((), ())), preferred_element_type=F32) * SCALE
            sc = jnp.where(seen, sc, NEG_BIG)
            old = part[o, 1, b]
            m_old, l_old = old[:, 0:1], old[:, HALF:HALF + 1]
            m_new = jnp.maximum(m_old, jnp.max(sc, axis=-1, keepdims=True))
            p = jnp.where(seen, jnp.exp(sc - m_new), 0.0)
            fade = jnp.exp(m_old - m_new)
            l_new = l_old * fade + jnp.sum(p, axis=-1, keepdims=True)
            part[o, 0, b] = part[o, 0, b] * fade + jnp.dot(p.astype(BF), stage[s, b, o, 1], preferred_element_type=F32)
            part[o, 1, b] = jnp.where(low, m_new, l_new)

    @pl.loop(0, BATCH)
    def _(b):
        attend(0, b)
        y_copy(b).wait_recv()
        xrecv[b] = norm_rows(xrecv[b].astype(F32), gain_a[...])

        @pl.loop(0, 2)
        def _(kv):
            for o in (2, 3, 1, 0):
                project(xrecv, 1, b, o, kv)
                out_copy(1, b, o, kv).start()

        attend(1, b)

    p_copy = [remote(part.at[d], precv.at[d - 1], p_s.at[d - 1], p_r.at[d - 1], (rep, near[d])) for d in (1, 2, 3)]
    for c in p_copy:
        c.start()
    for load in loads[4:]:
        load.wait()
    first = lax.broadcasted_iota(jnp.int32, (BATCH, 4, 1), 1) < 2
    s_self = jnp.where(first, jnp.sum(qall[0] * kself[...], axis=-1, keepdims=True) * SCALE, NEG_BIG)
    for c in p_copy:
        c.wait_recv()
    accs = [part[0, 0]] + [precv[i, 0] for i in range(3)]
    stats = [part[0, 1]] + [precv[i, 1] for i in range(3)]
    tops = [st[:, :, 0:1] for st in stats]
    top = s_self
    for t in tops:
        top = jnp.maximum(top, t)
    e_self = jnp.where(first, jnp.exp(s_self - top), 0.0)
    den = e_self
    num = e_self * vself[...]
    for t, st, ac in zip(tops, stats, accs):
        e = jnp.exp(t - top)
        den = den + e * st[:, :, HALF:HALF + 1]
        num = num + e * ac
    attn[...] = num / den
    for g in range(2):
        for h in range(2):
            flat[g * BATCH:(g + 1) * BATCH, h * HEAD_DIM:(h + 1) * HEAD_DIM] = attn[:, 2 * g + h, :]

    def reduce_columns(i, base):
        sends = [remote(psend.at[i, near[d]], rrecv.at[i, d - 1], r_s.at[i, d - 1], r_r.at[i, d - 1], (rep, near[d])) for d in range(1, 8)]
        for c in sends:
            c.start()
        total = psend[i, me]
        for d in range(1, 8):
            sends[d - 1].wait_recv()
            total = total + rrecv[i, d - 1]
        hid[i, me] = (base + total).astype(BF)
        gets = [remote(hid.at[i, me], hid.at[i, me], a_s.at[i, d - 1], a_r.at[i, d - 1], (rep, near[d])) for d in range(1, 8)]
        for c in gets:
            c.start()
        for d in range(1, 8):
            remote(hid.at[i, near[d]], hid.at[i, near[d]], a_s.at[i, d - 1], a_r.at[i, d - 1], (rep, near[d])).wait_recv()
        return sends + gets

    a16 = flat[...].astype(BF)
    for j in range(8):
        psend[0, j] = jnp.dot(a16, wob[:, j * SHARD:(j + 1) * SHARD], preferred_element_type=F32)
    mine = pl.ds(pl.multiple_of(me * SHARD, SHARD), SHARD)
    done = reduce_columns(0, rows[:, mine])

    sq = jnp.zeros((2 * BATCH, 1), F32)
    for j in range(8):
        hj = hid[0, j].astype(F32)
        sq = sq + jnp.sum(hj * hj, axis=-1, keepdims=True)
    inv = lax.rsqrt(sq / D_MODEL + 1e-5)
    for j in range(8):
        cols = slice(j * SHARD, (j + 1) * SHARD)
        norm2[:, cols] = (hid[0, j].astype(F32) * inv * gain_m[:, cols].astype(F32)).astype(BF)
    n2 = norm2[...]
    gate = jnp.dot(n2, wgb[...], preferred_element_type=F32)
    up = jnp.dot(n2, wub[...], preferred_element_type=F32)
    mid = (gate * jax.nn.sigmoid(gate) * up).astype(BF)
    for j in range(8):
        psend[1, j] = jnp.dot(mid, wdb[:, j * SHARD:(j + 1) * SHARD], preferred_element_type=F32)
    done += reduce_columns(1, hid[0, me].astype(F32))
    for j in range(8):
        cols = slice(j * SHARD, (j + 1) * SHARD)
        dec_out[:, cols] = hid[1, j][:BATCH]
        last_out[:, cols] = hid[1, j][BATCH:]

    for c in [w_x, w_s, w_z, w_xs, w_zs] + l_copy + q_copy + p_copy + done:
        c.wait_send()

    @pl.loop(0, BATCH)
    def _(b):
        y_copy(b).wait_send()
        for s in range(2):
            for kv in range(2):
                for o in range(4):
                    out_copy(s, b, o, kv).wait()


def layer(lens, prompt, new_tok, gain_a, gain_m, table, wq, wk, wv, wo, wg, wu, wd):
    vmem = pl.BlockSpec(memory_space=pltpu.VMEM)
    anym = pl.BlockSpec(memory_space=pl.ANY)
    dma = pltpu.SemaphoreType.DMA
    v = pltpu.VMEM
    return pl.pallas_call(
        layer_kernel,
        out_shape=(
            jax.ShapeDtypeStruct((2, BATCH, 8 * ROWS, HEAD_DIM), BF),
            jax.ShapeDtypeStruct((2, 2 * BATCH, HEAD_DIM), BF),
            jax.ShapeDtypeStruct((BATCH, D_MODEL), BF),
            jax.ShapeDtypeStruct((BATCH, D_MODEL), BF),
        ),
        in_specs=[pl.BlockSpec(memory_space=pltpu.SMEM), anym, vmem, vmem, vmem] + [anym] * 8,
        out_specs=(anym, vmem, vmem, vmem),
        scratch_shapes=[
            v((BATCH, SEQ_LOC, D_MODEL), BF), v((BATCH, SEQ_LOC, D_MODEL), BF), v((4, 2, D_MODEL, SHARD), BF),
            v((D_MODEL, SHARD), BF), v((SHARD, D_MODEL), BF), v((D_MODEL, FF_LOC), BF), v((D_MODEL, FF_LOC), BF), v((FF_LOC, D_MODEL), BF),
            v((TAB_ROWS, HEAD_DIM), F32), v((ROWS, HEAD_DIM), F32), v((2, BATCH, 4, 2, ROWS, HEAD_DIM), BF),
            v((BATCH, D_MODEL), F32), v((3, BATCH, D_MODEL), BF), v((3, BATCH, D_MODEL), BF), v((2 * BATCH, D_MODEL), F32),
            v((4, BATCH, 4, HEAD_DIM), F32), v((4, 2, BATCH, 4, HEAD_DIM), F32), v((3, 2, BATCH, 4, HEAD_DIM), F32),
            v((BATCH, 4, HEAD_DIM), F32), v((BATCH, 4, HEAD_DIM), F32), v((BATCH, 4, HEAD_DIM), F32), v((2 * BATCH, SHARD), F32),
            v((2, 8, 2 * BATCH, SHARD), F32), v((2, 7, 2 * BATCH, SHARD), F32), v((2, 8, 2 * BATCH, SHARD), BF), v((2 * BATCH, D_MODEL), BF),
            dma((8,)), dma((BATCH,)), dma((BATCH,)), dma((BATCH,)), dma((5,)), dma((5,)),
            dma((3, 2, BATCH, 2)), dma((3, 2, BATCH, 2)), dma((2, BATCH, 2)),
            dma((3,)), dma((3,)), dma((3,)), dma((3,)), dma((3,)), dma((3,)),
            dma((2, 7)), dma((2, 7)), dma((2, 7)), dma((2, 7)),
        ],
        compiler_params=pltpu.CompilerParams(collective_id=0, has_side_effects=True, vmem_limit_bytes=62 * 1024 * 1024),
        cost_estimate=pl.CostEstimate(flops=26_000_000_000, bytes_accessed=60_000_000, transcendentals=0),
        name='layer',
    )(lens, prompt, new_tok, gain_a, gain_m, table, wq, wk, wv, wo, wg, wu, wd)


def cache_kernel(kv, new, key_out, val_out, buf, row, load, store, row_sem):
    outs = (key_out, val_out)
    ins = [[pltpu.make_async_copy(kv.at[i, b], buf.at[i, b], load.at[i, b]) for b in range(BATCH)] for i in range(2)]
    rows_in = pltpu.make_async_copy(new, row, row_sem.at[0])
    rows_in.start()
    for i in range(2):
        for b in range(BATCH):
            ins[i][b].start()
    rows_in.wait()
    puts = [pltpu.make_async_copy(row.at[i], outs[i].at[0, :, pl.ds(SEQ_LEN, 1)], row_sem.at[1 + i]) for i in range(2)]
    for c in puts:
        c.start()
    for i in range(2):
        for b in range(BATCH):
            ins[i][b].wait()
            puts.append(pltpu.make_async_copy(buf.at[i, b], outs[i].at[0, b, pl.ds(0, SEQ_LEN)], store.at[i, b]))
            puts[-1].start()
    for c in puts:
        c.wait()


def caches(kv, new):
    anym = pl.BlockSpec(memory_space=pl.ANY)
    dma = pltpu.SemaphoreType.DMA
    shape = jax.ShapeDtypeStruct((1, BATCH, SEQ_LEN + 1, 2, HEAD_DIM), BF)
    return pl.pallas_call(
        cache_kernel,
        out_shape=(shape, shape),
        in_specs=[anym, anym],
        out_specs=(anym, anym),
        scratch_shapes=[
            pltpu.VMEM((2, BATCH, SEQ_LEN, 2, HEAD_DIM), BF), pltpu.VMEM((2, BATCH, 1, 2, HEAD_DIM), BF),
            dma((2, BATCH)), dma((2, BATCH)), dma((3,)),
        ],
        compiler_params=pltpu.CompilerParams(vmem_limit_bytes=62 * 1024 * 1024),
        cost_estimate=pl.CostEstimate(flops=0, bytes_accessed=50_000_000, transcendentals=0),
        name='caches',
    )(kv, new)


def solution(mesh):
    seq_spec = P('replica', 'model', None)
    col_spec = P(None, None, 'model')
    row_spec = P(None, 'model', None)
    gain_spec = P(None, None)
    tok_spec = P('replica', None)
    cache_spec = P(None, 'replica', None, 'model', None)
    in_specs = (seq_spec, P('replica'), tok_spec, gain_spec, col_spec, col_spec, col_spec, row_spec, gain_spec, col_spec, col_spec, row_spec)
    out_specs = (tok_spec, tok_spec, cache_spec, cache_spec)
    table = rope_table()

    def per_device(prompt, lengths, new_tok, norm_attn, w_q, w_k, w_v, w_o, norm_mlp, w_gate, w_up, w_down):
        kv, new, dec, last = layer(lengths, prompt, new_tok, norm_attn, norm_mlp, jnp.asarray(table), w_q, w_k, w_v, w_o, w_gate, w_up, w_down)
        keys, vals = caches(kv.reshape(2, BATCH, SEQ_LEN, 2, HEAD_DIM), new.reshape(2, BATCH, 1, 2, HEAD_DIM))
        return dec, last, keys, vals

    return jax.shard_map(per_device, mesh=mesh, in_specs=in_specs, out_specs=out_specs, check_vma=False)
```

time: 346 us -> 204 us (0.59)
  waiting for transfers between devices: 57 us -> 0 us
  other arithmetic: 40.4 us -> 0 us
  Pallas kernels: 172 us -> 202 us
  blocking collectives: 23.1 us -> 0 us
  matrix products: 21 us -> 0 us
  local copies, waits for them, and re-layouts: 17 us -> 1.24 us
  between operations: 14.3 us -> 0.68 us
    psum x2 -> x0, waiting for transfers between devices: 57 us -> none  [the longest x1 28.6 us: per_device(): hid = (rows.astype(f32) + lax.psum(attn_part, 'model')).astype(bf)]
    broadcast_in_dim x2 -> x0, other arithmetic: 33.8 us -> none  [the longest x1 16.9 us: per_device(): key_cache = jnp.concatenate([kv[0], k_new[:, None]], axis=1)[None]]
    pallas_call x1 -> x2, Pallas kernels: 172 us -> 202 us  [the longest x1 193 us: layer(): pl.pallas_call(layer_kernel, out_shape=(jax.ShapeDtypeStruct((2, BATCH, 8...]
    psum x1 -> x0, blocking collectives: 23.1 us -> none  [per_device(): last_row = lax.psum(last_part, 'model').astype(bf)]
    dot_general x9 -> x0, matrix products: 21 us -> none  [the longest x1 5.39 us: per_device(): mlp_part = jnp.dot(mid, w_down[0], preferred_element_type=f32)]
    slice x4 -> x0, local copies, waits for them, and re-layouts: 12.2 us -> none  [the longest x1 11.4 us: per_device(): kv[0]]
  transfers between devices with their start and end apart: 2 -> 0, of which waited for: 2 -> 0; matrix products, arithmetic and copies ran while one was open for 10% -> 0% of each run, Pallas kernels for 0% -> 0%
where the time goes in v2:
time: 204 us
  Pallas kernels  202 us (99%)
    pallas_call x1, Pallas kernels, layer(): pl.pallas_call(layer_kernel, out_shape=(jax.ShapeDtypeStruct((2, BATCH, 8...  193 us
    pallas_call x1, Pallas kernels, caches(): pl.pallas_call(cache_kernel, out_shape=(shape, shape), in_specs=[anym, an...  9.03 us

profile of v2, /device:TPU:0, one launch (start us, length us, event | category | flops | bytes accessed | tf_op | source)
XLA Modules:
  0.0 204.3 jit_solution(1391420110369267401)
XLA Ops:
  0.6 193.4 %layer.1 = (bf16[2,8,3072,128]{3,2,1,0:T(8,128)(2,1)}, bf16[2,16,128]{2,1,0:T(8,128)(2,1)}, bf16[8,2048]{1,0:T(8,128)(2,1)}, bf16[8,2048]{1,0:T(8,128)(2,1)}) custom-call(s32[8]{0:T(128)} %lens.1, bf16[8,192,2048]{2,1,0:T(8,128)(2,1)} %prompt.1, bf16[8,2048]{1,0:T(8,128)(2,1)} %new_tok.1, bf16[1,2048]{1,0:T(2,128)(2,1)} %gain_a.1, bf16[1,2048]{1,0:T(2,128)(2,1)} %gain_m.1, ...), custom_call_target="tpu_custom_call" | custom-call | flops 25999998976 | bytes 60000000 | tf_op jit(solution)/shard_map/layer/pallas_call | solution.py:335
  194.0 0.0 copy-start.1
  194.0 0.0 copy-start
  194.0 9.0 %caches.1 = (bf16[1,8,1537,2,128]{4,3,2,1,0:T(2,128)(2,1)}, bf16[1,8,1537,2,128]{4,3,2,1,0:T(2,128)(2,1)}) custom-call(bf16[2,8,1536,2,128]{4,3,2,1,0:T(2,128)(2,1)} %bitcast.2, bf16[2,8,1,2,128]{4,3,2,1,0:T(2,128)(2,1)} %bitcast.3), custom_call_target="tpu_custom_call" | custom-call | bytes 50000000 | tf_op jit(solution)/shard_map/caches/pallas_call | solution.py:389
  203.1 0.0 copy-done.1
  203.1 0.6 copy.19
  203.7 0.0 copy-done
  203.7 0.6 copy.20
Async XLA Ops:
  194.0 9.1 %copy-start.1 = (bf16[8,2048]{1,0:T(8,128)(2,1)S(1)}, bf16[8,2048]{1,0:T(8,128)(2,1)}, u32[]{:S(2)}) copy-start(bf16[8,2048]{1,0:T(8,128)(2,1)} %get-tuple-element.20) | copy-start | bytes 98308
  194.0 9.7 %copy-start = (bf16[8,2048]{1,0:T(8,128)(2,1)S(1)}, bf16[8,2048]{1,0:T(8,128)(2,1)}, u32[]{:S(2)}) copy-start(bf16[8,2048]{1,0:T(8,128)(2,1)} %get-tuple-element.21) | copy-start | bytes 98308

commit v3 on v2

--- a/solution.py
+++ b/solution.py
@@ -78,9 +78,14 @@
     loads = [pltpu.make_async_copy(a, b, lsem.at[i]) for i, (a, b) in enumerate((
         (wk.at[0], wbuf.at[0, 0]), (wv.at[0], wbuf.at[0, 1]), (table, tab), (wq.at[0], wqb), (wo.at[0], wob),
         (wg.at[0], wgb), (wu.at[0], wub), (wd.at[0], wdb)))]
+    for i, w in enumerate((wk, wv)):
+        @pl.when(rep == i)
+        def _():
+            remote(w.at[0], wbuf.at[2, rep], wsend.at[0], wrecv.at[0], (rep, xnb)).start()
+
+    y_copy(0).start()
     loads[0].start()
     loads[1].start()
-    y_copy(0).start()
 
     @pl.loop(0, BATCH)
     def _(b):
@@ -88,14 +93,13 @@
 
     for load in loads[2:]:
         load.start()
-    loads[0].wait()
-    loads[1].wait()
     w_x = remote(wbuf.at[0, rep], wbuf.at[2, rep], wsend.at[0], wrecv.at[0], (rep, xnb))
     w_s = remote(wbuf.at[0], wbuf.at[1], wsend.at[1], wrecv.at[1], (rep, sib))
     w_z = remote(wbuf.at[2, rep], wbuf.at[2, rep], wsend.at[2], wrecv.at[2], (znb, me))
     w_xs = remote(wbuf.at[2, rep], wbuf.at[3, rep], wsend.at[3], wrecv.at[3], (rep, sib))
     w_zs = remote(wbuf.at[2, znb], wbuf.at[3, znb], wsend.at[4], wrecv.at[4], (rep, sib))
-    w_x.start()
+    loads[0].wait()
+    loads[1].wait()
     w_s.start()
 
     def out_copy(s, b, o, kv):
@@ -162,17 +166,16 @@
     w_z.start()
     w_xs.start()
     l_copy[2].start()
-    w_xs.wait_recv()
-
-    def own_x_phase(kv):
+
+    def own_x_phase(kv, o):
         @pl.loop(0, BATCH)
         def _(b):
-            for o in (2, 3):
-                project(xbuf, 0, b, o, kv)
-            for o in (2, 3):
-                out_copy(0, b, o, kv).start()
-
-    own_x_phase(rep)
+            project(xbuf, 0, b, o, kv)
+            out_copy(0, b, o, kv).start()
+
+    own_x_phase(rep, 2)
+    w_xs.wait_recv()
+    own_x_phase(rep, 3)
 
     rows[0:BATCH, :] = new_tok[...].astype(F32)
     rows[BATCH:2 * BATCH, :] = join_last(2).astype(F32)
@@ -210,7 +213,8 @@
     w_z.wait_recv()
     w_zs.start()
     w_zs.wait_recv()
-    own_x_phase(znb)
+    own_x_phase(znb, 2)
+    own_x_phase(znb, 3)
     for c in q_copy:
         c.wait_recv()
 
@@ -232,23 +236,47 @@
             part[o, 0, b] = part[o, 0, b] * fade + jnp.dot(p.astype(BF), stage[s, b, o, 1], preferred_element_type=F32)
             part[o, 1, b] = jnp.where(low, m_new, l_new)
 
+    waiting = [(b, kv, o) for b in range(5, BATCH) for kv in range(2) for o in (2, 3)]
+
+    def leave(b, kv, o):
+        out_copy(1, b, o, kv).start()
+
     @pl.loop(0, BATCH)
     def _(b):
         attend(0, b)
         y_copy(b).wait_recv()
+
+        @pl.when(b == BATCH - 1)
+        def _():
+            for job in waiting[2:5]:
+                leave(*job)
         xrecv[b] = norm_rows(xrecv[b].astype(F32), gain_a[...])
 
         @pl.loop(0, 2)
         def _(kv):
-            for o in (2, 3, 1, 0):
+            for o in (2, 3):
+                project(xrecv, 1, b, o, kv)
+
+                @pl.when(b < 5)
+                def _():
+                    out_copy(1, b, o, kv).start()
+
+            for o in (1, 0):
                 project(xrecv, 1, b, o, kv)
                 out_copy(1, b, o, kv).start()
+
+        @pl.when(b == BATCH - 2)
+        def _():
+            for job in waiting[0:2]:
+                leave(*job)
 
         attend(1, b)
 
     p_copy = [remote(part.at[d], precv.at[d - 1], p_s.at[d - 1], p_r.at[d - 1], (rep, near[d])) for d in (1, 2, 3)]
     for c in p_copy:
         c.start()
+    for job in waiting[5:7]:
+        leave(*job)
     for load in loads[4:]:
         load.wait()
     first = lax.broadcasted_iota(jnp.int32, (BATCH, 4, 1), 1) < 2
@@ -273,10 +301,12 @@
         for h in range(2):
             flat[g * BATCH:(g + 1) * BATCH, h * HEAD_DIM:(h + 1) * HEAD_DIM] = attn[:, 2 * g + h, :]
 
-    def reduce_columns(i, base):
+    def reduce_columns(i, base, jobs):
         sends = [remote(psend.at[i, near[d]], rrecv.at[i, d - 1], r_s.at[i, d - 1], r_r.at[i, d - 1], (rep, near[d])) for d in range(1, 8)]
         for c in sends:
             c.start()
+        for job in jobs[0]:
+            leave(*job)
         total = psend[i, me]
         for d in range(1, 8):
             sends[d - 1].wait_recv()
@@ -285,6 +315,8 @@
         gets = [remote(hid.at[i, me], hid.at[i, me], a_s.at[i, d - 1], a_r.at[i, d - 1], (rep, near[d])) for d in range(1, 8)]
         for c in gets:
             c.start()
+        for job in jobs[1]:
+            leave(*job)
         for d in range(1, 8):
             remote(hid.at[i, near[d]], hid.at[i, near[d]], a_s.at[i, d - 1], a_r.at[i, d - 1], (rep, near[d])).wait_recv()
         return sends + gets
@@ -293,7 +325,7 @@
     for j in range(8):
         psend[0, j] = jnp.dot(a16, wob[:, j * SHARD:(j + 1) * SHARD], preferred_element_type=F32)
     mine = pl.ds(pl.multiple_of(me * SHARD, SHARD), SHARD)
-    done = reduce_columns(0, rows[:, mine])
+    done = reduce_columns(0, rows[:, mine], (waiting[7:8], waiting[8:11]))
 
     sq = jnp.zeros((2 * BATCH, 1), F32)
     for j in range(8):
@@ -309,7 +341,7 @@
     mid = (gate * jax.nn.sigmoid(gate) * up).astype(BF)
     for j in range(8):
         psend[1, j] = jnp.dot(mid, wdb[:, j * SHARD:(j + 1) * SHARD], preferred_element_type=F32)
-    done += reduce_columns(1, hid[0, me].astype(F32))
+    done += reduce_columns(1, hid[0, me].astype(F32), (waiting[11:12], ()))
     for j in range(8):
         cols = slice(j * SHARD, (j + 1) * SHARD)
         dec_out[:, cols] = hid[1, j][:BATCH]

time: 204 us -> 192 us (0.941)
  Pallas kernels: 202 us -> 190 us
    pallas_call x1, Pallas kernels: 193 us -> 181 us  [layer(): pl.pallas_call(layer_kernel, out_shape=(jax.ShapeDtypeStruct((2, BATCH, 8...]
where the time goes in v3:
time: 192 us
  Pallas kernels  190 us (99%)
    pallas_call x1, Pallas kernels, layer(): pl.pallas_call(layer_kernel, out_shape=(jax.ShapeDtypeStruct((2, BATCH, 8...  181 us
    pallas_call x1, Pallas kernels, caches(): pl.pallas_call(cache_kernel, out_shape=(shape, shape), in_specs=[anym, an...  9.03 us

profile of v3, /device:TPU:0, one launch (start us, length us, event | category | flops | bytes accessed | tf_op | source)
XLA Modules:
  0.0 192.1 jit_solution(11946363085987564363)
XLA Ops:
  0.6 181.1 %layer.1 = (bf16[2,8,3072,128]{3,2,1,0:T(8,128)(2,1)}, bf16[2,16,128]{2,1,0:T(8,128)(2,1)}, bf16[8,2048]{1,0:T(8,128)(2,1)}, bf16[8,2048]{1,0:T(8,128)(2,1)}) custom-call(s32[8]{0:T(128)} %lens.1, bf16[8,192,2048]{2,1,0:T(8,128)(2,1)} %prompt.1, bf16[8,2048]{1,0:T(8,128)(2,1)} %new_tok.1, bf16[1,2048]{1,0:T(2,128)(2,1)} %gain_a.1, bf16[1,2048]{1,0:T(2,128)(2,1)} %gain_m.1, ...), custom_call_target="tpu_custom_call" | custom-call | flops 25999998976 | bytes 60000000 | tf_op jit(solution)/shard_map/layer/pallas_call | solution.py:367
  181.8 0.0 copy-start.1
  181.8 0.0 copy-start
  181.8 9.0 %caches.1 = (bf16[1,8,1537,2,128]{4,3,2,1,0:T(2,128)(2,1)}, bf16[1,8,1537,2,128]{4,3,2,1,0:T(2,128)(2,1)}) custom-call(bf16[2,8,1536,2,128]{4,3,2,1,0:T(2,128)(2,1)} %bitcast.2, bf16[2,8,1,2,128]{4,3,2,1,0:T(2,128)(2,1)} %bitcast.3), custom_call_target="tpu_custom_call" | custom-call | bytes 50000000 | tf_op jit(solution)/shard_map/caches/pallas_call | solution.py:421
  190.8 0.0 copy-done.1
  190.8 0.6 copy.19
  191.5 0.0 copy-done
  191.5 0.6 copy.20
Async XLA Ops:
  181.8 9.1 %copy-start.1 = (bf16[8,2048]{1,0:T(8,128)(2,1)S(1)}, bf16[8,2048]{1,0:T(8,128)(2,1)}, u32[]{:S(2)}) copy-start(bf16[8,2048]{1,0:T(8,128)(2,1)} %get-tuple-element.20) | copy-start | bytes 98308
  181.8 9.7 %copy-start = (bf16[8,2048]{1,0:T(8,128)(2,1)S(1)}, bf16[8,2048]{1,0:T(8,128)(2,1)}, u32[]{:S(2)}) copy-start(bf16[8,2048]{1,0:T(8,128)(2,1)} %get-tuple-element.21) | copy-start | bytes 98308

commit v4 on v3

--- a/solution.py
+++ b/solution.py
@@ -248,8 +248,7 @@
 
         @pl.when(b == BATCH - 1)
         def _():
-            for job in waiting[2:5]:
-                leave(*job)
+            leave(*waiting[0])
         xrecv[b] = norm_rows(xrecv[b].astype(F32), gain_a[...])
 
         @pl.loop(0, 2)
@@ -265,17 +264,12 @@
                 project(xrecv, 1, b, o, kv)
                 out_copy(1, b, o, kv).start()
 
-        @pl.when(b == BATCH - 2)
-        def _():
-            for job in waiting[0:2]:
-                leave(*job)
-
         attend(1, b)
 
     p_copy = [remote(part.at[d], precv.at[d - 1], p_s.at[d - 1], p_r.at[d - 1], (rep, near[d])) for d in (1, 2, 3)]
     for c in p_copy:
         c.start()
-    for job in waiting[5:7]:
+    for job in waiting[1:3]:
         leave(*job)
     for load in loads[4:]:
         load.wait()
@@ -325,7 +319,7 @@
     for j in range(8):
         psend[0, j] = jnp.dot(a16, wob[:, j * SHARD:(j + 1) * SHARD], preferred_element_type=F32)
     mine = pl.ds(pl.multiple_of(me * SHARD, SHARD), SHARD)
-    done = reduce_columns(0, rows[:, mine], (waiting[7:8], waiting[8:11]))
+    done = reduce_columns(0, rows[:, mine], (waiting[3:5], waiting[5:8]))
 
     sq = jnp.zeros((2 * BATCH, 1), F32)
     for j in range(8):
@@ -341,7 +335,7 @@
     mid = (gate * jax.nn.sigmoid(gate) * up).astype(BF)
     for j in range(8):
         psend[1, j] = jnp.dot(mid, wdb[:, j * SHARD:(j + 1) * SHARD], preferred_element_type=F32)
-    done += reduce_columns(1, hid[0, me].astype(F32), (waiting[11:12], ()))
+    done += reduce_columns(1, hid[0, me].astype(F32), (waiting[8:10], waiting[10:12]))
     for j in range(8):
         cols = slice(j * SHARD, (j + 1) * SHARD)
         dec_out[:, cols] = hid[1, j][:BATCH]
@@ -393,7 +387,7 @@
     )(lens, prompt, new_tok, gain_a, gain_m, table, wq, wk, wv, wo, wg, wu, wd)
 
 
-def cache_kernel(kv, new, key_out, val_out, buf, row, load, store, row_sem):
+def cache_kernel(kv, new, dec, last, key_out, val_out, dec_out, last_out, buf, row, load, store, row_sem):
     outs = (key_out, val_out)
     ins = [[pltpu.make_async_copy(kv.at[i, b], buf.at[i, b], load.at[i, b]) for b in range(BATCH)] for i in range(2)]
     rows_in = pltpu.make_async_copy(new, row, row_sem.at[0])
@@ -401,6 +395,8 @@
     for i in range(2):
         for b in range(BATCH):
             ins[i][b].start()
+    dec_out[...] = dec[...]
+    last_out[...] = last[...]
     rows_in.wait()
     puts = [pltpu.make_async_copy(row.at[i], outs[i].at[0, :, pl.ds(SEQ_LEN, 1)], row_sem.at[1 + i]) for i in range(2)]
     for c in puts:
@@ -414,15 +410,17 @@
         c.wait()
 
 
-def caches(kv, new):
+def caches(kv, new, dec, last):
     anym = pl.BlockSpec(memory_space=pl.ANY)
     dma = pltpu.SemaphoreType.DMA
+    vmem = pl.BlockSpec(memory_space=pltpu.VMEM)
     shape = jax.ShapeDtypeStruct((1, BATCH, SEQ_LEN + 1, 2, HEAD_DIM), BF)
+    row = jax.ShapeDtypeStruct((BATCH, D_MODEL), BF)
     return pl.pallas_call(
         cache_kernel,
-        out_shape=(shape, shape),
-        in_specs=[anym, anym],
-        out_specs=(anym, anym),
+        out_shape=(shape, shape, row, row),
+        in_specs=[anym, anym, vmem, vmem],
+        out_specs=(anym, anym, vmem, vmem),
         scratch_shapes=[
             pltpu.VMEM((2, BATCH, SEQ_LEN, 2, HEAD_DIM), BF), pltpu.VMEM((2, BATCH, 1, 2, HEAD_DIM), BF),
             dma((2, BATCH)), dma((2, BATCH)), dma((3,)),
@@ -430,7 +428,7 @@
         compiler_params=pltpu.CompilerParams(vmem_limit_bytes=62 * 1024 * 1024),
         cost_estimate=pl.CostEstimate(flops=0, bytes_accessed=50_000_000, transcendentals=0),
         name='caches',
-    )(kv, new)
+    )(kv, new, dec, last)
 
 
 def solution(mesh):
@@ -446,7 +444,7 @@
 
     def per_device(prompt, lengths, new_tok, norm_attn, w_q, w_k, w_v, w_o, norm_mlp, w_gate, w_up, w_down):
         kv, new, dec, last = layer(lengths, prompt, new_tok, norm_attn, norm_mlp, jnp.asarray(table), w_q, w_k, w_v, w_o, w_gate, w_up, w_down)
-        keys, vals = caches(kv.reshape(2, BATCH, SEQ_LEN, 2, HEAD_DIM), new.reshape(2, BATCH, 1, 2, HEAD_DIM))
+        keys, vals, dec, last = caches(kv.reshape(2, BATCH, SEQ_LEN, 2, HEAD_DIM), new.reshape(2, BATCH, 1, 2, HEAD_DIM), dec, last)
         return dec, last, keys, vals
 
     return jax.shard_map(per_device, mesh=mesh, in_specs=in_specs, out_specs=out_specs, check_vma=False)

time: 192 us -> 193 us (level)
  Pallas kernels: 190 us -> 192 us
where the time goes in v4:
time: 193 us
  Pallas kernels  192 us (99%)
    pallas_call x1, Pallas kernels, layer(): pl.pallas_call(layer_kernel, out_shape=(jax.ShapeDtypeStruct((2, BATCH, 8...  182 us
    pallas_call x1, Pallas kernels, caches(): pl.pallas_call(cache_kernel, out_shape=(shape, shape, row, row), in_specs...  10.4 us

profile of v4, /device:TPU:0, one launch (start us, length us, event | category | flops | bytes accessed | tf_op | source)
XLA Modules:
  0.0 193.0 jit_solution(7270003319172616245)
XLA Ops:
  0.6 181.9 %layer.1 = (bf16[2,8,3072,128]{3,2,1,0:T(8,128)(2,1)}, bf16[2,16,128]{2,1,0:T(8,128)(2,1)}, bf16[8,2048]{1,0:T(8,128)(2,1)}, bf16[8,2048]{1,0:T(8,128)(2,1)}) custom-call(s32[8]{0:T(128)} %lens.1, bf16[8,192,2048]{2,1,0:T(8,128)(2,1)} %prompt.1, bf16[8,2048]{1,0:T(8,128)(2,1)} %new_tok.1, bf16[1,2048]{1,0:T(2,128)(2,1)} %gain_a.1, bf16[1,2048]{1,0:T(2,128)(2,1)} %gain_m.1, ...), custom_call_target="tpu_custom_call" | custom-call | flops 25999998976 | bytes 60000000 | tf_op jit(solution)/shard_map/layer/pallas_call | solution.py:361
  182.6 10.4 %caches.1 = (bf16[1,8,1537,2,128]{4,3,2,1,0:T(2,128)(2,1)}, bf16[1,8,1537,2,128]{4,3,2,1,0:T(2,128)(2,1)}, bf16[8,2048]{1,0:T(8,128)(2,1)}, bf16[8,2048]{1,0:T(8,128)(2,1)}) custom-call(bf16[2,8,1536,2,128]{4,3,2,1,0:T(2,128)(2,1)} %bitcast.2, bf16[2,8,1,2,128]{4,3,2,1,0:T(2,128)(2,1)} %bitcast.3, bf16[8,2048]{1,0:T(8,128)(2,1)} %get-tuple-element.14.dec, ...), custom_call_target="tpu_custom_call" | custom-call | bytes 50000000 | tf_op jit(solution)/shard_map/caches/pallas_call | solution.py:419

commit v5 on v4

--- a/solution.py
+++ b/solution.py
@@ -110,6 +110,14 @@
             return pltpu.make_async_copy(src, dst, ssem.at[s, b, kv])
         return remote(src, dst, osend.at[o - 1, s, b, kv], orecv.at[o - 1, s, b, kv], (rep, near[o]))
 
+    def own_two(b, o, kv):
+        dst = kv_out.at[kv, pl.ds(b, 2), pl.ds(pl.multiple_of(me * ROWS, ROWS), ROWS), :]
+        return remote(stage.at[0, pl.ds(b, 2), o, kv], dst, osend.at[o - 1, 0, b, kv], orecv.at[o - 1, 0, b, kv], (rep, near[o]))
+
+    def chunk_kv(b, o):
+        dst = kv_out.at[:, b, pl.ds(pl.multiple_of(ynb * ROWS, ROWS), ROWS), :]
+        return remote(stage.at[1, b, o], dst, osend.at[o - 1, 1, b, 0], orecv.at[o - 1, 1, b, 0], (rep, near[o]))
+
     def project(buf, s, b, o, kv):
         acc = jnp.dot(buf[b], wbuf[o, kv], preferred_element_type=F32)
         blk = me if s == 0 else ynb
@@ -168,10 +176,11 @@
     l_copy[2].start()
 
     def own_x_phase(kv, o):
-        @pl.loop(0, BATCH)
+        @pl.loop(0, BATCH, step=2)
         def _(b):
             project(xbuf, 0, b, o, kv)
-            out_copy(0, b, o, kv).start()
+            project(xbuf, 0, b + 1, o, kv)
+            own_two(b, o, kv).start()
 
     own_x_phase(rep, 2)
     w_xs.wait_recv()
@@ -256,9 +265,9 @@
             for o in (2, 3):
                 project(xrecv, 1, b, o, kv)
 
-                @pl.when(b < 5)
+                @pl.when((b < 5) & (kv == 1))
                 def _():
-                    out_copy(1, b, o, kv).start()
+                    chunk_kv(b, o).start()
 
             for o in (1, 0):
                 project(xrecv, 1, b, o, kv)
@@ -347,10 +356,23 @@
     @pl.loop(0, BATCH)
     def _(b):
         y_copy(b).wait_send()
-        for s in range(2):
+        for kv in range(2):
+            for s in range(2):
+                for o in (0, 1):
+                    out_copy(s, b, o, kv).wait()
+
+    for o in (2, 3):
+        @pl.loop(0, BATCH, step=2)
+        def _(b):
             for kv in range(2):
-                for o in range(4):
-                    out_copy(s, b, o, kv).wait()
+                own_two(b, o, kv).wait()
+
+        @pl.loop(0, 5)
+        def _(b):
+            chunk_kv(b, o).wait()
+
+    for b, kv, o in waiting:
+        out_copy(1, b, o, kv).wait()
 
 
 def layer(lens, prompt, new_tok, gain_a, gain_m, table, wq, wk, wv, wo, wg, wu, wd):

time: 193 us -> 193 us (level)
  no operation moved by 1% of the time
where the time goes in v5:
time: 193 us
  Pallas kernels  192 us (99%)
    pallas_call x1, Pallas kernels, layer(): pl.pallas_call(layer_kernel, out_shape=(jax.ShapeDtypeStruct((2, BATCH, 8...  182 us
    pallas_call x1, Pallas kernels, caches(): pl.pallas_call(cache_kernel, out_shape=(shape, shape, row, row), in_specs...  10.4 us

profile of v5, /device:TPU:0, one launch (start us, length us, event | category | flops | bytes accessed | tf_op | source)
XLA Modules:
  0.0 193.0 jit_solution(3590786366557127732)
XLA Ops:
  0.6 181.9 %layer.1 = (bf16[2,8,3072,128]{3,2,1,0:T(8,128)(2,1)}, bf16[2,16,128]{2,1,0:T(8,128)(2,1)}, bf16[8,2048]{1,0:T(8,128)(2,1)}, bf16[8,2048]{1,0:T(8,128)(2,1)}) custom-call(s32[8]{0:T(128)} %lens.1, bf16[8,192,2048]{2,1,0:T(8,128)(2,1)} %prompt.1, bf16[8,2048]{1,0:T(8,128)(2,1)} %new_tok.1, bf16[1,2048]{1,0:T(2,128)(2,1)} %gain_a.1, bf16[1,2048]{1,0:T(2,128)(2,1)} %gain_m.1, ...), custom_call_target="tpu_custom_call" | custom-call | flops 25999998976 | bytes 60000000 | tf_op jit(solution)/shard_map/layer/pallas_call | solution.py:383
  182.6 10.4 %caches.1 = (bf16[1,8,1537,2,128]{4,3,2,1,0:T(2,128)(2,1)}, bf16[1,8,1537,2,128]{4,3,2,1,0:T(2,128)(2,1)}, bf16[8,2048]{1,0:T(8,128)(2,1)}, bf16[8,2048]{1,0:T(8,128)(2,1)}) custom-call(bf16[2,8,1536,2,128]{4,3,2,1,0:T(2,128)(2,1)} %bitcast.2, bf16[2,8,1,2,128]{4,3,2,1,0:T(2,128)(2,1)} %bitcast.3, bf16[8,2048]{1,0:T(8,128)(2,1)} %get-tuple-element.14.dec, ...), custom_call_target="tpu_custom_call" | custom-call | bytes 50000000 | tf_op jit(solution)/shard_map/caches/pallas_call | solution.py:441

commit v6 on v5

--- a/solution.py
+++ b/solution.py
@@ -233,17 +233,19 @@
     def attend(s, b):
         blk = me if s == 0 else ynb
         seen = same_head & (blk * SEQ_LOC + lane // 2 < lens[b])
-        for o in range(4):
-            sc = lax.dot_general(qall[o, b].astype(BF), stage[s, b, o, 0], (((1,), (1,)), ((), ())), preferred_element_type=F32) * SCALE
-            sc = jnp.where(seen, sc, NEG_BIG)
-            old = part[o, 1, b]
-            m_old, l_old = old[:, 0:1], old[:, HALF:HALF + 1]
-            m_new = jnp.maximum(m_old, jnp.max(sc, axis=-1, keepdims=True))
-            p = jnp.where(seen, jnp.exp(sc - m_new), 0.0)
-            fade = jnp.exp(m_old - m_new)
-            l_new = l_old * fade + jnp.sum(p, axis=-1, keepdims=True)
-            part[o, 0, b] = part[o, 0, b] * fade + jnp.dot(p.astype(BF), stage[s, b, o, 1], preferred_element_type=F32)
-            part[o, 1, b] = jnp.where(low, m_new, l_new)
+        four = range(4)
+        old = [part[o, 1, b] for o in four]
+        acc = [part[o, 0, b] for o in four]
+        sc = [lax.dot_general(qall[o, b].astype(BF), stage[s, b, o, 0], (((1,), (1,)), ((), ())), preferred_element_type=F32) for o in four]
+        sc = [jnp.where(seen, x * SCALE, NEG_BIG) for x in sc]
+        top = [jnp.maximum(old[o][:, 0:1], jnp.max(sc[o], axis=-1, keepdims=True)) for o in four]
+        p = [jnp.where(seen, jnp.exp(sc[o] - top[o]), 0.0) for o in four]
+        fade = [jnp.exp(old[o][:, 0:1] - top[o]) for o in four]
+        den = [old[o][:, HALF:HALF + 1] * fade[o] + jnp.sum(p[o], axis=-1, keepdims=True) for o in four]
+        add = [jnp.dot(p[o].astype(BF), stage[s, b, o, 1], preferred_element_type=F32) for o in four]
+        for o in four:
+            part[o, 0, b] = acc[o] * fade[o] + add[o]
+            part[o, 1, b] = jnp.where(low, top[o], den[o])
 
     waiting = [(b, kv, o) for b in range(5, BATCH) for kv in range(2) for o in (2, 3)]
 
@@ -258,6 +260,7 @@
         @pl.when(b == BATCH - 1)
         def _():
             leave(*waiting[0])
+            leave(*waiting[1])
         xrecv[b] = norm_rows(xrecv[b].astype(F32), gain_a[...])
 
         @pl.loop(0, 2)
@@ -278,7 +281,7 @@
     p_copy = [remote(part.at[d], precv.at[d - 1], p_s.at[d - 1], p_r.at[d - 1], (rep, near[d])) for d in (1, 2, 3)]
     for c in p_copy:
         c.start()
-    for job in waiting[1:3]:
+    for job in waiting[2:4]:
         leave(*job)
     for load in loads[4:]:
         load.wait()
@@ -328,7 +331,7 @@
     for j in range(8):
         psend[0, j] = jnp.dot(a16, wob[:, j * SHARD:(j + 1) * SHARD], preferred_element_type=F32)
     mine = pl.ds(pl.multiple_of(me * SHARD, SHARD), SHARD)
-    done = reduce_columns(0, rows[:, mine], (waiting[3:5], waiting[5:8]))
+    done = reduce_columns(0, rows[:, mine], (waiting[4:6], waiting[6:8]))
 
     sq = jnp.zeros((2 * BATCH, 1), F32)
     for j in range(8):

time: 193 us -> 192 us (level)
  no operation moved by 1% of the time
where the time goes in v6:
time: 192 us
  Pallas kernels  191 us (99%)
    pallas_call x1, Pallas kernels, layer(): pl.pallas_call(layer_kernel, out_shape=(jax.ShapeDtypeStruct((2, BATCH, 8...  181 us
    pallas_call x1, Pallas kernels, caches(): pl.pallas_call(cache_kernel, out_shape=(shape, shape, row, row), in_specs...  10.4 us

profile of v6, /device:TPU:0, one launch (start us, length us, event | category | flops | bytes accessed | tf_op | source)
XLA Modules:
  0.0 191.9 jit_solution(8642087801775114973)
XLA Ops:
  0.6 180.8 %layer.1 = (bf16[2,8,3072,128]{3,2,1,0:T(8,128)(2,1)}, bf16[2,16,128]{2,1,0:T(8,128)(2,1)}, bf16[8,2048]{1,0:T(8,128)(2,1)}, bf16[8,2048]{1,0:T(8,128)(2,1)}) custom-call(s32[8]{0:T(128)} %lens.1, bf16[8,192,2048]{2,1,0:T(8,128)(2,1)} %prompt.1, bf16[8,2048]{1,0:T(8,128)(2,1)} %new_tok.1, bf16[1,2048]{1,0:T(2,128)(2,1)} %gain_a.1, bf16[1,2048]{1,0:T(2,128)(2,1)} %gain_m.1, ...), custom_call_target="tpu_custom_call" | custom-call | flops 25999998976 | bytes 60000000 | tf_op jit(solution)/shard_map/layer/pallas_call | solution.py:386
  181.5 10.4 %caches.1 = (bf16[1,8,1537,2,128]{4,3,2,1,0:T(2,128)(2,1)}, bf16[1,8,1537,2,128]{4,3,2,1,0:T(2,128)(2,1)}, bf16[8,2048]{1,0:T(8,128)(2,1)}, bf16[8,2048]{1,0:T(8,128)(2,1)}) custom-call(bf16[2,8,1536,2,128]{4,3,2,1,0:T(2,128)(2,1)} %bitcast.2, bf16[2,8,1,2,128]{4,3,2,1,0:T(2,128)(2,1)} %bitcast.3, bf16[8,2048]{1,0:T(8,128)(2,1)} %get-tuple-element.14.dec, ...), custom_call_target="tpu_custom_call" | custom-call | bytes 50000000 | tf_op jit(solution)/shard_map/caches/pallas_call | solution.py:444

commit v7 on v6

--- a/solution.py
+++ b/solution.py
@@ -49,7 +49,7 @@
                  xbuf, xrecv, wbuf, wqb, wob, wgb, wub, wdb, tab, tmp, stage,
                  lastf, lsend, lrecv, rows, qall, part, precv, kself, vself, attn, flat,
                  psend, rrecv, hid, norm2,
-                 lsem, xsem, ysend, yrecv, wsend, wrecv, osend, orecv, ssem,
+                 lsem, xsem, ysend, yrecv, wsend, wrecv, osend, orecv,
                  l_s, l_r, q_s, q_r, p_s, p_r, r_s, r_r, a_s, a_r):
     rep = lax.axis_index('replica')
     me = lax.axis_index('model')
@@ -105,18 +105,16 @@
     def out_copy(s, b, o, kv):
         blk = me if s == 0 else ynb
         dst = kv_out.at[kv, b, pl.ds(pl.multiple_of(blk * ROWS, ROWS), ROWS), :]
-        src = stage.at[s, b, o, kv]
-        if o == 0:
-            return pltpu.make_async_copy(src, dst, ssem.at[s, b, kv])
+        src = stage.at[s, b, o - 1, kv]
         return remote(src, dst, osend.at[o - 1, s, b, kv], orecv.at[o - 1, s, b, kv], (rep, near[o]))
 
     def own_two(b, o, kv):
         dst = kv_out.at[kv, pl.ds(b, 2), pl.ds(pl.multiple_of(me * ROWS, ROWS), ROWS), :]
-        return remote(stage.at[0, pl.ds(b, 2), o, kv], dst, osend.at[o - 1, 0, b, kv], orecv.at[o - 1, 0, b, kv], (rep, near[o]))
+        return remote(stage.at[0, pl.ds(b, 2), o - 1, kv], dst, osend.at[o - 1, 0, b, kv], orecv.at[o - 1, 0, b, kv], (rep, near[o]))
 
     def chunk_kv(b, o):
         dst = kv_out.at[:, b, pl.ds(pl.multiple_of(ynb * ROWS, ROWS), ROWS), :]
-        return remote(stage.at[1, b, o], dst, osend.at[o - 1, 1, b, 0], orecv.at[o - 1, 1, b, 0], (rep, near[o]))
+        return remote(stage.at[1, b, o - 1], dst, osend.at[o - 1, 1, b, 0], orecv.at[o - 1, 1, b, 0], (rep, near[o]))
 
     def project(buf, s, b, o, kv):
         acc = jnp.dot(buf[b], wbuf[o, kv], preferred_element_type=F32)
@@ -127,7 +125,10 @@
         sn = jnp.where(is_k, sn, 0.0)
         for h in range(2):
             tmp[pl.ds(h, SEQ_LOC, stride=2), :] = rotate(acc[:, h * HEAD_DIM:(h + 1) * HEAD_DIM], c, sn)
-        stage[s, b, o, kv] = tmp[...].astype(BF)
+        if o == 0:
+            kv_out[kv, b, pl.ds(pl.multiple_of(blk * ROWS, ROWS), ROWS), :] = tmp[...].astype(BF)
+        else:
+            stage[s, b, o - 1, kv] = tmp[...].astype(BF)
 
     @pl.loop(0, BATCH)
     def _(b):
@@ -151,7 +152,6 @@
         @pl.loop(0, 2)
         def _(kv):
             project(xbuf, 0, b, 0, kv)
-            out_copy(0, b, 0, kv).start()
 
     def join_last(i):
         l_copy[i].wait_recv()
@@ -234,15 +234,17 @@
         blk = me if s == 0 else ynb
         seen = same_head & (blk * SEQ_LOC + lane // 2 < lens[b])
         four = range(4)
+        mine = pl.ds(pl.multiple_of(blk * ROWS, ROWS), ROWS)
+        keys, vals = ([kv_out[kv, b, mine, :]] + [stage[s, b, o - 1, kv] for o in (1, 2, 3)] for kv in range(2))
         old = [part[o, 1, b] for o in four]
         acc = [part[o, 0, b] for o in four]
-        sc = [lax.dot_general(qall[o, b].astype(BF), stage[s, b, o, 0], (((1,), (1,)), ((), ())), preferred_element_type=F32) for o in four]
+        sc = [lax.dot_general(qall[o, b].astype(BF), keys[o], (((1,), (1,)), ((), ())), preferred_element_type=F32) for o in four]
         sc = [jnp.where(seen, x * SCALE, NEG_BIG) for x in sc]
         top = [jnp.maximum(old[o][:, 0:1], jnp.max(sc[o], axis=-1, keepdims=True)) for o in four]
         p = [jnp.where(seen, jnp.exp(sc[o] - top[o]), 0.0) for o in four]
         fade = [jnp.exp(old[o][:, 0:1] - top[o]) for o in four]
         den = [old[o][:, HALF:HALF + 1] * fade[o] + jnp.sum(p[o], axis=-1, keepdims=True) for o in four]
-        add = [jnp.dot(p[o].astype(BF), stage[s, b, o, 1], preferred_element_type=F32) for o in four]
+        add = [jnp.dot(p[o].astype(BF), vals[o], preferred_element_type=F32) for o in four]
         for o in four:
             part[o, 0, b] = acc[o] * fade[o] + add[o]
             part[o, 1, b] = jnp.where(low, top[o], den[o])
@@ -272,9 +274,9 @@
                 def _():
                     chunk_kv(b, o).start()
 
-            for o in (1, 0):
-                project(xrecv, 1, b, o, kv)
-                out_copy(1, b, o, kv).start()
+            project(xrecv, 1, b, 1, kv)
+            out_copy(1, b, 1, kv).start()
+            project(xrecv, 1, b, 0, kv)
 
         attend(1, b)
 
@@ -361,8 +363,7 @@
         y_copy(b).wait_send()
         for kv in range(2):
             for s in range(2):
-                for o in (0, 1):
-                    out_copy(s, b, o, kv).wait()
+                out_copy(s, b, 1, kv).wait()
 
     for o in (2, 3):
         @pl.loop(0, BATCH, step=2)
@@ -386,51 +387,44 @@
     return pl.pallas_call(
         layer_kernel,
         out_shape=(
-            jax.ShapeDtypeStruct((2, BATCH, 8 * ROWS, HEAD_DIM), BF),
-            jax.ShapeDtypeStruct((2, 2 * BATCH, HEAD_DIM), BF),
-            jax.ShapeDtypeStruct((BATCH, D_MODEL), BF),
-            jax.ShapeDtypeStruct((BATCH, D_MODEL), BF),
+            pltpu.VMEM((2, BATCH, 8 * ROWS, HEAD_DIM), BF),
+            pltpu.VMEM((2, 2 * BATCH, HEAD_DIM), BF),
+            pltpu.VMEM((BATCH, D_MODEL), BF),
+            pltpu.VMEM((BATCH, D_MODEL), BF),
         ),
         in_specs=[pl.BlockSpec(memory_space=pltpu.SMEM), anym, vmem, vmem, vmem] + [anym] * 8,
-        out_specs=(anym, vmem, vmem, vmem),
+        out_specs=(vmem, vmem, vmem, vmem),
         scratch_shapes=[
             v((BATCH, SEQ_LOC, D_MODEL), BF), v((BATCH, SEQ_LOC, D_MODEL), BF), v((4, 2, D_MODEL, SHARD), BF),
             v((D_MODEL, SHARD), BF), v((SHARD, D_MODEL), BF), v((D_MODEL, FF_LOC), BF), v((D_MODEL, FF_LOC), BF), v((FF_LOC, D_MODEL), BF),
-            v((TAB_ROWS, HEAD_DIM), F32), v((ROWS, HEAD_DIM), F32), v((2, BATCH, 4, 2, ROWS, HEAD_DIM), BF),
+            v((TAB_ROWS, HEAD_DIM), F32), v((ROWS, HEAD_DIM), F32), v((2, BATCH, 3, 2, ROWS, HEAD_DIM), BF),
             v((BATCH, D_MODEL), F32), v((3, BATCH, D_MODEL), BF), v((3, BATCH, D_MODEL), BF), v((2 * BATCH, D_MODEL), F32),
             v((4, BATCH, 4, HEAD_DIM), F32), v((4, 2, BATCH, 4, HEAD_DIM), F32), v((3, 2, BATCH, 4, HEAD_DIM), F32),
             v((BATCH, 4, HEAD_DIM), F32), v((BATCH, 4, HEAD_DIM), F32), v((BATCH, 4, HEAD_DIM), F32), v((2 * BATCH, SHARD), F32),
             v((2, 8, 2 * BATCH, SHARD), F32), v((2, 7, 2 * BATCH, SHARD), F32), v((2, 8, 2 * BATCH, SHARD), BF), v((2 * BATCH, D_MODEL), BF),
             dma((8,)), dma((BATCH,)), dma((BATCH,)), dma((BATCH,)), dma((5,)), dma((5,)),
-            dma((3, 2, BATCH, 2)), dma((3, 2, BATCH, 2)), dma((2, BATCH, 2)),
+            dma((3, 2, BATCH, 2)), dma((3, 2, BATCH, 2)),
             dma((3,)), dma((3,)), dma((3,)), dma((3,)), dma((3,)), dma((3,)),
             dma((2, 7)), dma((2, 7)), dma((2, 7)), dma((2, 7)),
         ],
-        compiler_params=pltpu.CompilerParams(collective_id=0, has_side_effects=True, vmem_limit_bytes=62 * 1024 * 1024),
+        compiler_params=pltpu.CompilerParams(collective_id=0, has_side_effects=True, vmem_limit_bytes=49 * 1024 * 1024),
         cost_estimate=pl.CostEstimate(flops=26_000_000_000, bytes_accessed=60_000_000, transcendentals=0),
         name='layer',
     )(lens, prompt, new_tok, gain_a, gain_m, table, wq, wk, wv, wo, wg, wu, wd)
 
 
-def cache_kernel(kv, new, dec, last, key_out, val_out, dec_out, last_out, buf, row, load, store, row_sem):
+def cache_kernel(kv, new, dec, last, key_out, val_out, dec_out, last_out, store, row_sem):
     outs = (key_out, val_out)
-    ins = [[pltpu.make_async_copy(kv.at[i, b], buf.at[i, b], load.at[i, b]) for b in range(BATCH)] for i in range(2)]
-    rows_in = pltpu.make_async_copy(new, row, row_sem.at[0])
-    rows_in.start()
+    puts = []
     for i in range(2):
         for b in range(BATCH):
-            ins[i][b].start()
+            puts.append(pltpu.make_async_copy(kv.at[i, b], outs[i].at[0, b, pl.ds(0, SEQ_LEN)], store.at[i, b]))
+            puts[-1].start()
+    for i in range(2):
+        puts.append(pltpu.make_async_copy(new.at[i], outs[i].at[0, :, pl.ds(SEQ_LEN, 1)], row_sem.at[i]))
+        puts[-1].start()
     dec_out[...] = dec[...]
     last_out[...] = last[...]
-    rows_in.wait()
-    puts = [pltpu.make_async_copy(row.at[i], outs[i].at[0, :, pl.ds(SEQ_LEN, 1)], row_sem.at[1 + i]) for i in range(2)]
-    for c in puts:
-        c.start()
-    for i in range(2):
-        for b in range(BATCH):
-            ins[i][b].wait()
-            puts.append(pltpu.make_async_copy(buf.at[i, b], outs[i].at[0, b, pl.ds(0, SEQ_LEN)], store.at[i, b]))
-            puts[-1].start()
     for c in puts:
         c.wait()
 
@@ -446,12 +440,9 @@
         out_shape=(shape, shape, row, row),
         in_specs=[anym, anym, vmem, vmem],
         out_specs=(anym, anym, vmem, vmem),
-        scratch_shapes=[
-            pltpu.VMEM((2, BATCH, SEQ_LEN, 2, HEAD_DIM), BF), pltpu.VMEM((2, BATCH, 1, 2, HEAD_DIM), BF),
-            dma((2, BATCH)), dma((2, BATCH)), dma((3,)),
-        ],
-        compiler_params=pltpu.CompilerParams(vmem_limit_bytes=62 * 1024 * 1024),
-        cost_estimate=pl.CostEstimate(flops=0, bytes_accessed=50_000_000, transcendentals=0),
+        scratch_shapes=[dma((2, BATCH)), dma((2,))],
+        compiler_params=pltpu.CompilerParams(vmem_limit_bytes=4 * 1024 * 1024),
+        cost_estimate=pl.CostEstimate(flops=0, bytes_accessed=13_000_000, transcendentals=0),
         name='caches',
     )(kv, new, dec, last)
 

time: 192 us -> 186 us (0.969)
  Pallas kernels: 191 us -> 185 us
    pallas_call x1, Pallas kernels: 10.4 us -> 5.35 us  [caches(): pl.pallas_call(cache_kernel, out_shape=(shape, shape, row, row), in_specs...]
where the time goes in v7:
time: 186 us
  Pallas kernels  185 us (99%)
    pallas_call x1, Pallas kernels, layer(): pl.pallas_call(layer_kernel, out_shape=(pltpu.VMEM((2, BATCH, 8 * ROWS, H...  180 us
    pallas_call x1, Pallas kernels, caches(): pl.pallas_call(cache_kernel, out_shape=(shape, shape, row, row), in_specs...  5.35 us

profile of v7, /device:TPU:0, one launch (start us, length us, event | category | flops | bytes accessed | tf_op | source)
XLA Modules:
  0.0 185.9 jit_solution(4076304263144029383)
XLA Ops:
  0.6 179.9 %layer.1 = (bf16[2,8,3072,128]{3,2,1,0:T(8,128)(2,1)S(1)}, bf16[2,16,128]{2,1,0:T(8,128)(2,1)S(1)}, bf16[8,2048]{1,0:T(8,128)(2,1)S(1)}, bf16[8,2048]{1,0:T(8,128)(2,1)S(1)}) custom-call(s32[8]{0:T(128)} %lens.1, bf16[8,192,2048]{2,1,0:T(8,128)(2,1)} %prompt.1, bf16[8,2048]{1,0:T(8,128)(2,1)} %new_tok.1, bf16[1,2048]{1,0:T(2,128)(2,1)} %gain_a.1, ...), custom_call_target="tpu_custom_call" | custom-call | flops 25999998976 | bytes 60000000 | tf_op jit(solution)/shard_map/layer/pallas_call | solution.py:387
  180.5 5.3 %caches.1 = (bf16[1,8,1537,2,128]{4,3,2,1,0:T(2,128)(2,1)}, bf16[1,8,1537,2,128]{4,3,2,1,0:T(2,128)(2,1)}, bf16[8,2048]{1,0:T(8,128)(2,1)}, bf16[8,2048]{1,0:T(8,128)(2,1)}) custom-call(bf16[2,8,1536,2,128]{4,3,2,1,0:T(2,128)(2,1)S(1)} %bitcast.2, bf16[2,8,1,2,128]{4,3,2,1,0:T(2,128)(2,1)S(1)} %bitcast.3, bf16[8,2048]{1,0:T(8,128)(2,1)S(1)} %get-tuple-element.14.dec, ...), custom_call_target="tpu_custom_call" | custom-call | bytes 13000000 | tf_op jit(solution)/shard_map/caches/pallas_call | solution.py:438

commit v8 on v7

--- a/solution.py
+++ b/solution.py
@@ -249,7 +249,7 @@
             part[o, 0, b] = acc[o] * fade[o] + add[o]
             part[o, 1, b] = jnp.where(low, top[o], den[o])
 
-    waiting = [(b, kv, o) for b in range(5, BATCH) for kv in range(2) for o in (2, 3)]
+    waiting = [(b, kv, o) for b in range(6, BATCH) for kv in range(2) for o in (2, 3)]
 
     def leave(b, kv, o):
         out_copy(1, b, o, kv).start()
@@ -259,10 +259,6 @@
         attend(0, b)
         y_copy(b).wait_recv()
 
-        @pl.when(b == BATCH - 1)
-        def _():
-            leave(*waiting[0])
-            leave(*waiting[1])
         xrecv[b] = norm_rows(xrecv[b].astype(F32), gain_a[...])
 
         @pl.loop(0, 2)
@@ -270,7 +266,7 @@
             for o in (2, 3):
                 project(xrecv, 1, b, o, kv)
 
-                @pl.when((b < 5) & (kv == 1))
+                @pl.when((b < 6) & (kv == 1))
                 def _():
                     chunk_kv(b, o).start()
 
@@ -283,7 +279,7 @@
     p_copy = [remote(part.at[d], precv.at[d - 1], p_s.at[d - 1], p_r.at[d - 1], (rep, near[d])) for d in (1, 2, 3)]
     for c in p_copy:
         c.start()
-    for job in waiting[2:4]:
+    for job in waiting[0:2]:
         leave(*job)
     for load in loads[4:]:
         load.wait()
@@ -333,7 +329,7 @@
     for j in range(8):
         psend[0, j] = jnp.dot(a16, wob[:, j * SHARD:(j + 1) * SHARD], preferred_element_type=F32)
     mine = pl.ds(pl.multiple_of(me * SHARD, SHARD), SHARD)
-    done = reduce_columns(0, rows[:, mine], (waiting[4:6], waiting[6:8]))
+    done = reduce_columns(0, rows[:, mine], (waiting[2:3], waiting[3:6]))
 
     sq = jnp.zeros((2 * BATCH, 1), F32)
     for j in range(8):
@@ -349,7 +345,7 @@
     mid = (gate * jax.nn.sigmoid(gate) * up).astype(BF)
     for j in range(8):
         psend[1, j] = jnp.dot(mid, wdb[:, j * SHARD:(j + 1) * SHARD], preferred_element_type=F32)
-    done += reduce_columns(1, hid[0, me].astype(F32), (waiting[8:10], waiting[10:12]))
+    done += reduce_columns(1, hid[0, me].astype(F32), (waiting[6:7], waiting[7:8]))
     for j in range(8):
         cols = slice(j * SHARD, (j + 1) * SHARD)
         dec_out[:, cols] = hid[1, j][:BATCH]
@@ -371,7 +367,7 @@
             for kv in range(2):
                 own_two(b, o, kv).wait()
 
-        @pl.loop(0, 5)
+        @pl.loop(0, 6)
         def _(b):
             chunk_kv(b, o).wait()
 

time: 186 us -> 185 us (level)
  no operation moved by 1% of the time
where the time goes in v8:
time: 185 us
  Pallas kernels  184 us (99%)
    pallas_call x1, Pallas kernels, layer(): pl.pallas_call(layer_kernel, out_shape=(pltpu.VMEM((2, BATCH, 8 * ROWS, H...  179 us
    pallas_call x1, Pallas kernels, caches(): pl.pallas_call(cache_kernel, out_shape=(shape, shape, row, row), in_specs...  5.35 us

profile of v8, /device:TPU:0, one launch (start us, length us, event | category | flops | bytes accessed | tf_op | source)
XLA Modules:
  0.0 185.1 jit_solution(10862853840038345165)
XLA Ops:
  0.6 179.1 %layer.1 = (bf16[2,8,3072,128]{3,2,1,0:T(8,128)(2,1)S(1)}, bf16[2,16,128]{2,1,0:T(8,128)(2,1)S(1)}, bf16[8,2048]{1,0:T(8,128)(2,1)S(1)}, bf16[8,2048]{1,0:T(8,128)(2,1)S(1)}) custom-call(s32[8]{0:T(128)} %lens.1, bf16[8,192,2048]{2,1,0:T(8,128)(2,1)} %prompt.1, bf16[8,2048]{1,0:T(8,128)(2,1)} %new_tok.1, bf16[1,2048]{1,0:T(2,128)(2,1)} %gain_a.1, ...), custom_call_target="tpu_custom_call" | custom-call | flops 25999998976 | bytes 60000000 | tf_op jit(solution)/shard_map/layer/pallas_call | solution.py:383
  179.7 5.3 %caches.1 = (bf16[1,8,1537,2,128]{4,3,2,1,0:T(2,128)(2,1)}, bf16[1,8,1537,2,128]{4,3,2,1,0:T(2,128)(2,1)}, bf16[8,2048]{1,0:T(8,128)(2,1)}, bf16[8,2048]{1,0:T(8,128)(2,1)}) custom-call(bf16[2,8,1536,2,128]{4,3,2,1,0:T(2,128)(2,1)S(1)} %bitcast.2, bf16[2,8,1,2,128]{4,3,2,1,0:T(2,128)(2,1)S(1)} %bitcast.3, bf16[8,2048]{1,0:T(8,128)(2,1)S(1)} %get-tuple-element.14.dec, ...), custom_call_target="tpu_custom_call" | custom-call | bytes 13000000 | tf_op jit(solution)/shard_map/caches/pallas_call | solution.py:434

commit v9 on v8

--- a/solution.py
+++ b/solution.py
@@ -279,6 +279,8 @@
     p_copy = [remote(part.at[d], precv.at[d - 1], p_s.at[d - 1], p_r.at[d - 1], (rep, near[d])) for d in (1, 2, 3)]
     for c in p_copy:
         c.start()
+    for c in p_copy:
+        c.wait_send()
     for job in waiting[0:2]:
         leave(*job)
     for load in loads[4:]:
@@ -309,6 +311,8 @@
         sends = [remote(psend.at[i, near[d]], rrecv.at[i, d - 1], r_s.at[i, d - 1], r_r.at[i, d - 1], (rep, near[d])) for d in range(1, 8)]
         for c in sends:
             c.start()
+        for c in sends:
+            c.wait_send()
         for job in jobs[0]:
             leave(*job)
         total = psend[i, me]
@@ -319,17 +323,18 @@
         gets = [remote(hid.at[i, me], hid.at[i, me], a_s.at[i, d - 1], a_r.at[i, d - 1], (rep, near[d])) for d in range(1, 8)]
         for c in gets:
             c.start()
+        for c in gets:
+            c.wait_send()
         for job in jobs[1]:
             leave(*job)
         for d in range(1, 8):
             remote(hid.at[i, near[d]], hid.at[i, near[d]], a_s.at[i, d - 1], a_r.at[i, d - 1], (rep, near[d])).wait_recv()
-        return sends + gets
 
     a16 = flat[...].astype(BF)
     for j in range(8):
         psend[0, j] = jnp.dot(a16, wob[:, j * SHARD:(j + 1) * SHARD], preferred_element_type=F32)
     mine = pl.ds(pl.multiple_of(me * SHARD, SHARD), SHARD)
-    done = reduce_columns(0, rows[:, mine], (waiting[2:3], waiting[3:6]))
+    reduce_columns(0, rows[:, mine], (waiting[2:3], waiting[3:6]))
 
     sq = jnp.zeros((2 * BATCH, 1), F32)
     for j in range(8):
@@ -345,13 +350,13 @@
     mid = (gate * jax.nn.sigmoid(gate) * up).astype(BF)
     for j in range(8):
         psend[1, j] = jnp.dot(mid, wdb[:, j * SHARD:(j + 1) * SHARD], preferred_element_type=F32)
-    done += reduce_columns(1, hid[0, me].astype(F32), (waiting[6:7], waiting[7:8]))
+    reduce_columns(1, hid[0, me].astype(F32), (waiting[6:7], waiting[7:8]))
     for j in range(8):
         cols = slice(j * SHARD, (j + 1) * SHARD)
         dec_out[:, cols] = hid[1, j][:BATCH]
         last_out[:, cols] = hid[1, j][BATCH:]
 
-    for c in [w_x, w_s, w_z, w_xs, w_zs] + l_copy + q_copy + p_copy + done:
+    for c in [w_x, w_s, w_z, w_xs, w_zs] + l_copy + q_copy:
         c.wait_send()
 
     @pl.loop(0, BATCH)

time: 185 us -> 186 us (level)
  no operation moved by 1% of the time
where the time goes in v9:
time: 186 us
  Pallas kernels  185 us (99%)
    pallas_call x1, Pallas kernels, layer(): pl.pallas_call(layer_kernel, out_shape=(pltpu.VMEM((2, BATCH, 8 * ROWS, H...  180 us
    pallas_call x1, Pallas kernels, caches(): pl.pallas_call(cache_kernel, out_shape=(shape, shape, row, row), in_specs...  5.35 us

profile of v9, /device:TPU:0, one launch (start us, length us, event | category | flops | bytes accessed | tf_op | source)
XLA Modules:
  0.0 185.8 jit_solution(11625218043897841860)
XLA Ops:
  0.6 179.8 %layer.1 = (bf16[2,8,3072,128]{3,2,1,0:T(8,128)(2,1)S(1)}, bf16[2,16,128]{2,1,0:T(8,128)(2,1)S(1)}, bf16[8,2048]{1,0:T(8,128)(2,1)S(1)}, bf16[8,2048]{1,0:T(8,128)(2,1)S(1)}) custom-call(s32[8]{0:T(128)} %lens.1, bf16[8,192,2048]{2,1,0:T(8,128)(2,1)} %prompt.1, bf16[8,2048]{1,0:T(8,128)(2,1)} %new_tok.1, bf16[1,2048]{1,0:T(2,128)(2,1)} %gain_a.1, ...), custom_call_target="tpu_custom_call" | custom-call | flops 25999998976 | bytes 60000000 | tf_op jit(solution)/shard_map/layer/pallas_call | solution.py:388
  180.4 5.3 %caches.1 = (bf16[1,8,1537,2,128]{4,3,2,1,0:T(2,128)(2,1)}, bf16[1,8,1537,2,128]{4,3,2,1,0:T(2,128)(2,1)}, bf16[8,2048]{1,0:T(8,128)(2,1)}, bf16[8,2048]{1,0:T(8,128)(2,1)}) custom-call(bf16[2,8,1536,2,128]{4,3,2,1,0:T(2,128)(2,1)S(1)} %bitcast.2, bf16[2,8,1,2,128]{4,3,2,1,0:T(2,128)(2,1)S(1)} %bitcast.3, bf16[8,2048]{1,0:T(8,128)(2,1)S(1)} %get-tuple-element.14.dec, ...), custom_call_target="tpu_custom_call" | custom-call | bytes 13000000 | tf_op jit(solution)/shard_map/caches/pallas_call | solution.py:439

commit v10 on v8

--- a/solution.py
+++ b/solution.py
@@ -48,7 +48,7 @@
                  kv_out, new_out, dec_out, last_out,
                  xbuf, xrecv, wbuf, wqb, wob, wgb, wub, wdb, tab, tmp, stage,
                  lastf, lsend, lrecv, rows, qall, part, precv, kself, vself, attn, flat,
-                 psend, rrecv, hid, norm2,
+                 psend, rrecv, rsum, base2, hid, norm2,
                  lsem, xsem, ysend, yrecv, wsend, wrecv, osend, orecv,
                  l_s, l_r, q_s, q_r, p_s, p_r, r_s, r_r, a_s, a_r):
     rep = lax.axis_index('replica')
@@ -279,7 +279,7 @@
     p_copy = [remote(part.at[d], precv.at[d - 1], p_s.at[d - 1], p_r.at[d - 1], (rep, near[d])) for d in (1, 2, 3)]
     for c in p_copy:
         c.start()
-    for job in waiting[0:2]:
+    for job in waiting[0:4]:
         leave(*job)
     for load in loads[4:]:
         load.wait()
@@ -305,31 +305,42 @@
         for h in range(2):
             flat[g * BATCH:(g + 1) * BATCH, h * HEAD_DIM:(h + 1) * HEAD_DIM] = attn[:, 2 * g + h, :]
 
+    def quarter(flip):
+        yy, cc = (ypos, 1 - ypos)[flip >> 2], (core, 1 - core)[flip & 1]
+        return pl.ds(4 * yy + 2 * cc, 2)
+
+    side = (1, 4, 5)
+
     def reduce_columns(i, base, jobs):
-        sends = [remote(psend.at[i, near[d]], rrecv.at[i, d - 1], r_s.at[i, d - 1], r_r.at[i, d - 1], (rep, near[d])) for d in range(1, 8)]
+        sends = [remote(psend.at[i, quarter(d)], rrecv.at[i, k], r_s.at[i, k], r_r.at[i, k], (rep, near[d])) for k, d in enumerate(side)]
         for c in sends:
             c.start()
-        for job in jobs[0]:
+        total = psend[i, quarter(0)]
+        for k in range(3):
+            sends[k].wait_recv()
+            total = total + rrecv[i, k]
+        rsum[i] = total
+        cross = remote(rsum.at[i], rrecv.at[i, 3], r_s.at[i, 3], r_r.at[i, 3], (rep, xnb))
+        cross.start()
+        for job in jobs:
             leave(*job)
-        total = psend[i, me]
-        for d in range(1, 8):
-            sends[d - 1].wait_recv()
-            total = total + rrecv[i, d - 1]
-        hid[i, me] = (base + total).astype(BF)
-        gets = [remote(hid.at[i, me], hid.at[i, me], a_s.at[i, d - 1], a_r.at[i, d - 1], (rep, near[d])) for d in range(1, 8)]
+        cross.wait_recv()
+        total = total + rrecv[i, 3]
+        hid[i, quarter(0)] = (base + total).astype(BF)
+        gets = [remote(hid.at[i, quarter(0)], hid.at[i, quarter(0)], a_s.at[i, k], a_r.at[i, k], (rep, near[d])) for k, d in enumerate(side)]
         for c in gets:
             c.start()
-        for job in jobs[1]:
-            leave(*job)
-        for d in range(1, 8):
-            remote(hid.at[i, near[d]], hid.at[i, near[d]], a_s.at[i, d - 1], a_r.at[i, d - 1], (rep, near[d])).wait_recv()
-        return sends + gets
+        for k, d in enumerate(side):
+            remote(hid.at[i, quarter(d)], hid.at[i, quarter(d)], a_s.at[i, k], a_r.at[i, k], (rep, near[d])).wait_recv()
+        return sends + [cross] + gets
 
     a16 = flat[...].astype(BF)
     for j in range(8):
         psend[0, j] = jnp.dot(a16, wob[:, j * SHARD:(j + 1) * SHARD], preferred_element_type=F32)
-    mine = pl.ds(pl.multiple_of(me * SHARD, SHARD), SHARD)
-    done = reduce_columns(0, rows[:, mine], (waiting[2:3], waiting[3:6]))
+    for k in range(2):
+        cols = pl.ds(pl.multiple_of((4 * ypos + 2 * core + k) * SHARD, SHARD), SHARD)
+        base2[k] = rows[:, cols]
+    done = reduce_columns(0, base2[...], waiting[4:8])
 
     sq = jnp.zeros((2 * BATCH, 1), F32)
     for j in range(8):
@@ -345,7 +356,7 @@
     mid = (gate * jax.nn.sigmoid(gate) * up).astype(BF)
     for j in range(8):
         psend[1, j] = jnp.dot(mid, wdb[:, j * SHARD:(j + 1) * SHARD], preferred_element_type=F32)
-    done += reduce_columns(1, hid[0, me].astype(F32), (waiting[6:7], waiting[7:8]))
+    done += reduce_columns(1, hid[0, quarter(0)].astype(F32), ())
     for j in range(8):
         cols = slice(j * SHARD, (j + 1) * SHARD)
         dec_out[:, cols] = hid[1, j][:BATCH]
@@ -397,11 +408,11 @@
             v((BATCH, D_MODEL), F32), v((3, BATCH, D_MODEL), BF), v((3, BATCH, D_MODEL), BF), v((2 * BATCH, D_MODEL), F32),
             v((4, BATCH, 4, HEAD_DIM), F32), v((4, 2, BATCH, 4, HEAD_DIM), F32), v((3, 2, BATCH, 4, HEAD_DIM), F32),
             v((BATCH, 4, HEAD_DIM), F32), v((BATCH, 4, HEAD_DIM), F32), v((BATCH, 4, HEAD_DIM), F32), v((2 * BATCH, SHARD), F32),
-            v((2, 8, 2 * BATCH, SHARD), F32), v((2, 7, 2 * BATCH, SHARD), F32), v((2, 8, 2 * BATCH, SHARD), BF), v((2 * BATCH, D_MODEL), BF),
+            v((2, 8, 2 * BATCH, SHARD), F32), v((2, 4, 2, 2 * BATCH, SHARD), F32), v((2, 2, 2 * BATCH, SHARD), F32), v((2, 2 * BATCH, SHARD), F32), v((2, 8, 2 * BATCH, SHARD), BF), v((2 * BATCH, D_MODEL), BF),
             dma((8,)), dma((BATCH,)), dma((BATCH,)), dma((BATCH,)), dma((5,)), dma((5,)),
             dma((3, 2, BATCH, 2)), dma((3, 2, BATCH, 2)),
             dma((3,)), dma((3,)), dma((3,)), dma((3,)), dma((3,)), dma((3,)),
-            dma((2, 7)), dma((2, 7)), dma((2, 7)), dma((2, 7)),
+            dma((2, 4)), dma((2, 4)), dma((2, 3)), dma((2, 3)),
         ],
         compiler_params=pltpu.CompilerParams(collective_id=0, has_side_effects=True, vmem_limit_bytes=49 * 1024 * 1024),
         cost_estimate=pl.CostEstimate(flops=26_000_000_000, bytes_accessed=60_000_000, transcendentals=0),

time: 185 us -> 188 us (1.016)
  Pallas kernels: 184 us -> 187 us
    pallas_call x1, Pallas kernels: 179 us -> 181 us  [layer(): pl.pallas_call(layer_kernel, out_shape=(pltpu.VMEM((2, BATCH, 8 * ROWS, H...]
where the time goes in v10:
time: 188 us; the launch traced here: 187 us
  Pallas kernels  187 us (99%)
    pallas_call x1, Pallas kernels, layer(): pl.pallas_call(layer_kernel, out_shape=(pltpu.VMEM((2, BATCH, 8 * ROWS, H...  181 us
    pallas_call x1, Pallas kernels, caches(): pl.pallas_call(cache_kernel, out_shape=(shape, shape, row, row), in_specs...  5.35 us

profile of v10, /device:TPU:0, one launch (start us, length us, event | category | flops | bytes accessed | tf_op | source)
XLA Modules:
  0.0 187.4 jit_solution(914699674739939597)
XLA Ops:
  0.6 181.4 %layer.1 = (bf16[2,8,3072,128]{3,2,1,0:T(8,128)(2,1)S(1)}, bf16[2,16,128]{2,1,0:T(8,128)(2,1)S(1)}, bf16[8,2048]{1,0:T(8,128)(2,1)S(1)}, bf16[8,2048]{1,0:T(8,128)(2,1)S(1)}) custom-call(s32[8]{0:T(128)} %lens.1, bf16[8,192,2048]{2,1,0:T(8,128)(2,1)} %prompt.1, bf16[8,2048]{1,0:T(8,128)(2,1)} %new_tok.1, bf16[1,2048]{1,0:T(2,128)(2,1)} %gain_a.1, ...), custom_call_target="tpu_custom_call" | custom-call | flops 25999998976 | bytes 60000000 | tf_op jit(solution)/shard_map/layer/pallas_call | solution.py:394
  182.1 5.3 %caches.1 = (bf16[1,8,1537,2,128]{4,3,2,1,0:T(2,128)(2,1)}, bf16[1,8,1537,2,128]{4,3,2,1,0:T(2,128)(2,1)}, bf16[8,2048]{1,0:T(8,128)(2,1)}, bf16[8,2048]{1,0:T(8,128)(2,1)}) custom-call(bf16[2,8,1536,2,128]{4,3,2,1,0:T(2,128)(2,1)S(1)} %bitcast.2, bf16[2,8,1,2,128]{4,3,2,1,0:T(2,128)(2,1)S(1)} %bitcast.3, bf16[8,2048]{1,0:T(8,128)(2,1)S(1)} %get-tuple-element.14.dec, ...), custom_call_target="tpu_custom_call" | custom-call | bytes 13000000 | tf_op jit(solution)/shard_map/caches/pallas_call | solution.py:445

commit v11 on v8

--- a/solution.py
+++ b/solution.py
@@ -133,14 +133,11 @@
     @pl.loop(0, BATCH)
     def _(b):
         x_load(b).wait()
-        x = xbuf[b].astype(F32)
         here = me * SEQ_LOC + lax.broadcasted_iota(jnp.int32, (SEQ_LOC, 1), 0) == lens[b] - 1
-        lastf[pl.ds(b, 1), :] = jnp.sum(jnp.where(here, x, 0.0), axis=0, keepdims=True)
-        xbuf[b] = norm_rows(x, gain_a[...])
+        lastf[pl.ds(b, 1), :] = jnp.sum(jnp.where(here, xbuf[b].astype(F32), 0.0), axis=0, keepdims=True)
 
     l_copy = [remote(lsend.at[i], lrecv.at[i], l_s.at[i], l_r.at[i], (rep, near[d])) for i, d in enumerate((4, 1, 2))]
     lsend[0] = lastf[...].astype(BF)
-    loads[2].wait()
     l_copy[0].start()
 
     @pl.loop(1, BATCH)
@@ -149,30 +146,20 @@
 
     @pl.loop(0, BATCH)
     def _(b):
-        @pl.loop(0, 2)
-        def _(kv):
-            project(xbuf, 0, b, 0, kv)
+        xbuf[b] = norm_rows(xbuf[b].astype(F32), gain_a[...])
 
     def join_last(i):
         l_copy[i].wait_recv()
         return (lsend[i].astype(F32) + lrecv[i].astype(F32)).astype(BF)
 
     lsend[1] = join_last(0)
-    w_s.wait_recv()
     l_copy[1].start()
-
-    @pl.loop(0, BATCH)
-    def _(b):
-        @pl.loop(0, 2)
-        def _(kv):
-            project(xbuf, 0, b, 1, kv)
-            out_copy(0, b, 1, kv).start()
-
-    lsend[2] = join_last(1)
+    loads[2].wait()
 
     w_x.wait_recv()
     w_z.start()
     w_xs.start()
+    lsend[2] = join_last(1)
     l_copy[2].start()
 
     def own_x_phase(kv, o):
@@ -219,6 +206,16 @@
     for c in q_copy:
         c.start()
 
+    w_s.wait_recv()
+
+    @pl.loop(0, BATCH)
+    def _(b):
+        @pl.loop(0, 2)
+        def _(kv):
+            project(xbuf, 0, b, 0, kv)
+            project(xbuf, 0, b, 1, kv)
+            out_copy(0, b, 1, kv).start()
+
     w_z.wait_recv()
     w_zs.start()
     w_zs.wait_recv()

time: 185 us -> 183 us (0.989)
  Pallas kernels: 184 us -> 182 us
    pallas_call x1, Pallas kernels: 179 us -> 177 us  [layer(): pl.pallas_call(layer_kernel, out_shape=(pltpu.VMEM((2, BATCH, 8 * ROWS, H...]
where the time goes in v11:
time: 183 us
  Pallas kernels  182 us (99%)
    pallas_call x1, Pallas kernels, layer(): pl.pallas_call(layer_kernel, out_shape=(pltpu.VMEM((2, BATCH, 8 * ROWS, H...  177 us
    pallas_call x1, Pallas kernels, caches(): pl.pallas_call(cache_kernel, out_shape=(shape, shape, row, row), in_specs...  5.35 us

profile of v11, /device:TPU:0, one launch (start us, length us, event | category | flops | bytes accessed | tf_op | source)
XLA Modules:
  0.0 182.8 jit_solution(10219635895755363358)
XLA Ops:
  0.6 176.8 %layer.1 = (bf16[2,8,3072,128]{3,2,1,0:T(8,128)(2,1)S(1)}, bf16[2,16,128]{2,1,0:T(8,128)(2,1)S(1)}, bf16[8,2048]{1,0:T(8,128)(2,1)S(1)}, bf16[8,2048]{1,0:T(8,128)(2,1)S(1)}) custom-call(s32[8]{0:T(128)} %lens.1, bf16[8,192,2048]{2,1,0:T(8,128)(2,1)} %prompt.1, bf16[8,2048]{1,0:T(8,128)(2,1)} %new_tok.1, bf16[1,2048]{1,0:T(2,128)(2,1)} %gain_a.1, ...), custom_call_target="tpu_custom_call" | custom-call | flops 25999998976 | bytes 60000000 | tf_op jit(solution)/shard_map/layer/pallas_call | solution.py:380
  177.4 5.3 %caches.1 = (bf16[1,8,1537,2,128]{4,3,2,1,0:T(2,128)(2,1)}, bf16[1,8,1537,2,128]{4,3,2,1,0:T(2,128)(2,1)}, bf16[8,2048]{1,0:T(8,128)(2,1)}, bf16[8,2048]{1,0:T(8,128)(2,1)}) custom-call(bf16[2,8,1536,2,128]{4,3,2,1,0:T(2,128)(2,1)S(1)} %bitcast.2, bf16[2,8,1,2,128]{4,3,2,1,0:T(2,128)(2,1)S(1)} %bitcast.3, bf16[8,2048]{1,0:T(8,128)(2,1)S(1)} %get-tuple-element.14.dec, ...), custom_call_target="tpu_custom_call" | custom-call | bytes 13000000 | tf_op jit(solution)/shard_map/caches/pallas_call | solution.py:431

commit v12 on v11

--- a/solution.py
+++ b/solution.py
@@ -139,14 +139,15 @@
     l_copy = [remote(lsend.at[i], lrecv.at[i], l_s.at[i], l_r.at[i], (rep, near[d])) for i, d in enumerate((4, 1, 2))]
     lsend[0] = lastf[...].astype(BF)
     l_copy[0].start()
-
-    @pl.loop(1, BATCH)
-    def _(b):
-        y_copy(b).start()
+    y_copy(1).start()
 
     @pl.loop(0, BATCH)
     def _(b):
         xbuf[b] = norm_rows(xbuf[b].astype(F32), gain_a[...])
+
+    @pl.loop(2, BATCH)
+    def _(b):
+        remote(xbuf.at[b], xrecv.at[b], ysend.at[b], yrecv.at[b], (rep, ynb)).start()
 
     def join_last(i):
         l_copy[i].wait_recv()
@@ -256,7 +257,9 @@
         attend(0, b)
         y_copy(b).wait_recv()
 
-        xrecv[b] = norm_rows(xrecv[b].astype(F32), gain_a[...])
+        @pl.when(b < 2)
+        def _():
+            xrecv[b] = norm_rows(xrecv[b].astype(F32), gain_a[...])
 
         @pl.loop(0, 2)
         def _(kv):

time: 183 us -> 183 us (level)
  no operation moved by 1% of the time
where the time goes in v12:
time: 183 us
  Pallas kernels  182 us (99%)
    pallas_call x1, Pallas kernels, layer(): pl.pallas_call(layer_kernel, out_shape=(pltpu.VMEM((2, BATCH, 8 * ROWS, H...  177 us
    pallas_call x1, Pallas kernels, caches(): pl.pallas_call(cache_kernel, out_shape=(shape, shape, row, row), in_specs...  5.35 us

profile of v12, /device:TPU:0, one launch (start us, length us, event | category | flops | bytes accessed | tf_op | source)
XLA Modules:
  0.0 182.8 jit_solution(847895709661986995)
XLA Ops:
  0.6 176.8 %layer.1 = (bf16[2,8,3072,128]{3,2,1,0:T(8,128)(2,1)S(1)}, bf16[2,16,128]{2,1,0:T(8,128)(2,1)S(1)}, bf16[8,2048]{1,0:T(8,128)(2,1)S(1)}, bf16[8,2048]{1,0:T(8,128)(2,1)S(1)}) custom-call(s32[8]{0:T(128)} %lens.1, bf16[8,192,2048]{2,1,0:T(8,128)(2,1)} %prompt.1, bf16[8,2048]{1,0:T(8,128)(2,1)} %new_tok.1, bf16[1,2048]{1,0:T(2,128)(2,1)} %gain_a.1, ...), custom_call_target="tpu_custom_call" | custom-call | flops 25999998976 | bytes 60000000 | tf_op jit(solution)/shard_map/layer/pallas_call | solution.py:383
  177.4 5.3 %caches.1 = (bf16[1,8,1537,2,128]{4,3,2,1,0:T(2,128)(2,1)}, bf16[1,8,1537,2,128]{4,3,2,1,0:T(2,128)(2,1)}, bf16[8,2048]{1,0:T(8,128)(2,1)}, bf16[8,2048]{1,0:T(8,128)(2,1)}) custom-call(bf16[2,8,1536,2,128]{4,3,2,1,0:T(2,128)(2,1)S(1)} %bitcast.2, bf16[2,8,1,2,128]{4,3,2,1,0:T(2,128)(2,1)S(1)} %bitcast.3, bf16[8,2048]{1,0:T(8,128)(2,1)S(1)} %get-tuple-element.14.dec, ...), custom_call_target="tpu_custom_call" | custom-call | bytes 13000000 | tf_op jit(solution)/shard_map/caches/pallas_call | solution.py:434

commit v13 on v12

--- a/solution.py
+++ b/solution.py
@@ -247,7 +247,7 @@
             part[o, 0, b] = acc[o] * fade[o] + add[o]
             part[o, 1, b] = jnp.where(low, top[o], den[o])
 
-    waiting = [(b, kv, o) for b in range(6, BATCH) for kv in range(2) for o in (2, 3)]
+    waiting = [(b, kv, o) for b in range(5, BATCH) for kv in range(2) for o in (2, 3)]
 
     def leave(b, kv, o):
         out_copy(1, b, o, kv).start()
@@ -266,7 +266,7 @@
             for o in (2, 3):
                 project(xrecv, 1, b, o, kv)
 
-                @pl.when((b < 6) & (kv == 1))
+                @pl.when((b < 5) & (kv == 1))
                 def _():
                     chunk_kv(b, o).start()
 
@@ -279,7 +279,7 @@
     p_copy = [remote(part.at[d], precv.at[d - 1], p_s.at[d - 1], p_r.at[d - 1], (rep, near[d])) for d in (1, 2, 3)]
     for c in p_copy:
         c.start()
-    for job in waiting[0:2]:
+    for job in waiting[0:3]:
         leave(*job)
     for load in loads[4:]:
         load.wait()
@@ -329,7 +329,7 @@
     for j in range(8):
         psend[0, j] = jnp.dot(a16, wob[:, j * SHARD:(j + 1) * SHARD], preferred_element_type=F32)
     mine = pl.ds(pl.multiple_of(me * SHARD, SHARD), SHARD)
-    done = reduce_columns(0, rows[:, mine], (waiting[2:3], waiting[3:6]))
+    done = reduce_columns(0, rows[:, mine], (waiting[3:5], waiting[5:8]))
 
     sq = jnp.zeros((2 * BATCH, 1), F32)
     for j in range(8):
@@ -345,7 +345,7 @@
     mid = (gate * jax.nn.sigmoid(gate) * up).astype(BF)
     for j in range(8):
         psend[1, j] = jnp.dot(mid, wdb[:, j * SHARD:(j + 1) * SHARD], preferred_element_type=F32)
-    done += reduce_columns(1, hid[0, me].astype(F32), (waiting[6:7], waiting[7:8]))
+    done += reduce_columns(1, hid[0, me].astype(F32), (waiting[8:10], waiting[10:12]))
     for j in range(8):
         cols = slice(j * SHARD, (j + 1) * SHARD)
         dec_out[:, cols] = hid[1, j][:BATCH]
@@ -367,7 +367,7 @@
             for kv in range(2):
                 own_two(b, o, kv).wait()
 
-        @pl.loop(0, 6)
+        @pl.loop(0, 5)
         def _(b):
             chunk_kv(b, o).wait()
 

time: 183 us -> 188 us (1.027)
  Pallas kernels: 182 us -> 187 us
    pallas_call x1, Pallas kernels: 177 us -> 182 us  [layer(): pl.pallas_call(layer_kernel, out_shape=(pltpu.VMEM((2, BATCH, 8 * ROWS, H...]
where the time goes in v13:
time: 188 us
  Pallas kernels  187 us (99%)
    pallas_call x1, Pallas kernels, layer(): pl.pallas_call(layer_kernel, out_shape=(pltpu.VMEM((2, BATCH, 8 * ROWS, H...  182 us
    pallas_call x1, Pallas kernels, caches(): pl.pallas_call(cache_kernel, out_shape=(shape, shape, row, row), in_specs...  5.35 us

profile of v13, /device:TPU:0, one launch (start us, length us, event | category | flops | bytes accessed | tf_op | source)
XLA Modules:
  0.0 187.9 jit_solution(3771750897359579559)
XLA Ops:
  0.6 181.9 %layer.1 = (bf16[2,8,3072,128]{3,2,1,0:T(8,128)(2,1)S(1)}, bf16[2,16,128]{2,1,0:T(8,128)(2,1)S(1)}, bf16[8,2048]{1,0:T(8,128)(2,1)S(1)}, bf16[8,2048]{1,0:T(8,128)(2,1)S(1)}) custom-call(s32[8]{0:T(128)} %lens.1, bf16[8,192,2048]{2,1,0:T(8,128)(2,1)} %prompt.1, bf16[8,2048]{1,0:T(8,128)(2,1)} %new_tok.1, bf16[1,2048]{1,0:T(2,128)(2,1)} %gain_a.1, ...), custom_call_target="tpu_custom_call" | custom-call | flops 25999998976 | bytes 60000000 | tf_op jit(solution)/shard_map/layer/pallas_call | solution.py:383
  182.6 5.3 %caches.1 = (bf16[1,8,1537,2,128]{4,3,2,1,0:T(2,128)(2,1)}, bf16[1,8,1537,2,128]{4,3,2,1,0:T(2,128)(2,1)}, bf16[8,2048]{1,0:T(8,128)(2,1)}, bf16[8,2048]{1,0:T(8,128)(2,1)}) custom-call(bf16[2,8,1536,2,128]{4,3,2,1,0:T(2,128)(2,1)S(1)} %bitcast.2, bf16[2,8,1,2,128]{4,3,2,1,0:T(2,128)(2,1)S(1)} %bitcast.3, bf16[8,2048]{1,0:T(8,128)(2,1)S(1)} %get-tuple-element.14.dec, ...), custom_call_target="tpu_custom_call" | custom-call | bytes 13000000 | tf_op jit(solution)/shard_map/caches/pallas_call | solution.py:434
